TPU v7x, 512 devices: a whole 4x4x16 slice. The times are simulated.
512 devices in a mesh: seq: 64 (over z, y), head: 8 (over x, core).
Axes of the slice: x: 4, y: 4, z: 16, core: 2. Of those that a mesh axis runs over, the one named last changes fastest.
Arguments:
- hidden_state_input: bfloat16 [16, 8192], P(None, 'seq'), may hold values from -40 to 40
- attention_norm_gain: bfloat16 [8192], P('seq'), may hold values from 0.099609375 to 1.8984375
- query_projection_matrix: bfloat16 [8192, 8192], P('seq', 'head'), may hold values from -0.0625 to 0.0625
- key_projection_matrix: bfloat16 [8192, 1024], P('seq', 'head'), may hold values from -0.0625 to 0.0625
- value_projection_matrix: bfloat16 [8192, 1024], P('seq', 'head'), may hold values from -0.0625 to 0.0625
- output_projection_matrix: bfloat16 [8192, 8192], P('head', 'seq'), may hold values from -0.25 to 0.25
- adapter_down_matrix: bfloat16 [512, 16, 8192], P('head', None, 'seq'), may hold values from -0.0625 to 0.0625
- adapter_up_matrix: bfloat16 [512, 16, 8192], P('seq', None, 'head'), may hold values from -3 to 3
- adapter_choice_index: int32 [16], replicated, may hold values from 0 to 511
- lengths: int32 [16], replicated, may hold values from 4 to 16384
- rotated_key_cache: bfloat16 [16, 16384, 8, 128], P(None, 'seq', 'head'), may hold values from -200 to 200
- cached_value_rows: bfloat16 [16, 16384, 8, 128], P(None, 'seq', 'head'), may hold values from -24 to 24
Outputs:
- output_sum: bfloat16 [16, 8192], P(None, 'seq')
Inputs may be any that keep to these rules, and one draw needn't show every extreme that they name: `adapter_choice_index`: index of the adapter that serves each request. The new token stands at position lengths[r]; cache entries at lengths[r] and beyond are not read.
All inputs are finite; a program needn't handle non-finite values.
Results may differ from a plain program's by a relative error of at most 0.025.
Values may be sent and summed in bfloat16 or wider, within the bound.
A program may use at most 64 MiB of HBM per device.

v0:
```python
import jax
import jax.numpy as jnp
from jax import lax
from jax.sharding import Mesh
from jax.sharding import PartitionSpec as P

SEQ = ("seq_0", "seq_1")
HEAD = ("head_0", "head_1")


norm_epsilon = 1e-05
adapter_scale_factor = 1.0
rope_base = 500000.0
masked_score = -1e30


def sent_to_all(value, axis):
    copies = jnp.broadcast_to(value, (lax.axis_size(axis), *value.shape))
    return lax.all_to_all(copies, axis, split_axis=0, concat_axis=0, tiled=True)


def taken_together(value, axis):
    everything = sent_to_all(value, axis)
    return jnp.sum(everything, axis=0)


def one_axis_at_a_time(value, axes):
    far, near = axes
    return taken_together(taken_together(value, near), far)


def in_one(arrays, axis):
    ends = [0]
    for a in arrays:
        ends.append(ends[-1] + a.size)
    subtotal = one_axis_at_a_time(jnp.concatenate([a.ravel() for a in arrays]), axis)
    return tuple((subtotal[b:e].reshape(a.shape) for a, b, e in zip(arrays, ends, ends[1:])))


def cut_along(value, dim, devices):
    lengths = value.shape
    pieces = value.reshape(*lengths[:dim], devices, lengths[dim] // devices, *lengths[dim + 1 :])
    return jnp.moveaxis(pieces, dim, 0)


def sum_at_owner(value, axis, dim):
    pieces = cut_along(value, dim, lax.axis_size(axis))
    arrived = lax.all_to_all(pieces, axis, split_axis=0, concat_axis=0, tiled=True)
    return arrived.sum(axis=0)


def filled_up(lines, devices):
    spare = -len(lines) % devices
    return jnp.pad(lines, [(0, spare)] + [(0, 0)] * (lines.ndim - 1))


def laid_out(pieces, dim):
    lengths = list(pieces.shape[1:])
    lengths[dim] *= pieces.shape[0]
    return jnp.moveaxis(pieces, 0, dim).reshape(lengths)


def gathered_copies(value, axis, dim):
    pieces = sent_to_all(value, axis)
    return laid_out(pieces, dim)


def total_of(value, axes):
    own = sum_at_owner(filled_up(value, lax.axis_size(axes)), axes, 0)
    whole = gathered_copies(own, axes, 0)
    return whole[: len(value)].reshape(value.shape)


def in_one_2(arrays, axis):
    vector, at, finished = (jnp.concatenate([a.reshape(-1) for a in arrays]), 0, [])
    subtotal = total_of(vector, axis)
    for a in arrays:
        finished.append(subtotal[at : at + a.size].reshape(a.shape))
        at += a.size
    return tuple(finished)


def all_in_one(value, axis):
    leaves = jax.tree.leaves(value)
    order = sorted(range(len(leaves)), key=lambda k: -leaves[k].size)
    width = (1, *leaves[order[0]].shape)[-1]
    lines = [
        jnp.pad(leaves[k].reshape(-1), (0, -leaves[k].size % width)).reshape(-1, width)
        for k in order
    ]
    both, at, found = (lax.all_gather(jnp.concatenate(lines), axis), 0, {})
    for k, line in zip(order, lines):
        share = both[:, at : at + len(line)].reshape(len(both), -1)
        found[k] = share[:, : leaves[k].size].reshape(-1, *leaves[k].shape)
        at += len(line)
    numbers = iter(range(len(leaves)))
    return jax.tree.map(lambda _: found[next(numbers)], value)


def merged_by_axis(value, axes, combine):
    for axis in axes:
        pieces = all_in_one(
            jax.tree.map(
                lambda part, kind: part.astype(kind),
                value,
                (jnp.bfloat16, jnp.bfloat16, jnp.bfloat16),
            ),
            axis,
        )
        widened = [
            jax.tree.map(lambda part, own: part[k].astype(own.dtype), pieces, value)
            for k in range(lax.axis_size(axis))
        ]
        value = widened[0]
        for partner_block in widened[1:]:
            value = combine(value, partner_block)
    return value


def rotate(vectors, positions):
    half_dim = vectors.shape[-1] // 2
    frequency = jnp.exp(
        -jnp.arange(half_dim, dtype=jnp.float32) * (jnp.log(jnp.float32(rope_base)) / half_dim)
    )
    angles = positions.astype(jnp.float32)[:, None] * frequency[None, :]
    cosine = jnp.cos(angles)[:, None, :]
    sine_val = jnp.sin(angles)[:, None, :]
    lower_half = vectors[..., :half_dim]
    upper_half = vectors[..., half_dim:]
    return jnp.concatenate(
        [lower_half * cosine - upper_half * sine_val, upper_half * cosine + lower_half * sine_val],
        axis=-1,
    )


def combine_parts(earlier, later):
    max_one, sum_one, out_one = earlier
    max_two, sum_two, out_two = later
    overall = jnp.maximum(max_one, max_two)
    scale_one = jnp.exp(max_one - overall)
    scale_two = jnp.exp(max_two - overall)
    return (
        overall,
        sum_one * scale_one + sum_two * scale_two,
        out_one * scale_one[..., None] + out_two * scale_two[..., None],
    )


def body(
    hidden_state_input,
    attention_norm_gain,
    query_projection_matrix,
    key_projection_matrix,
    value_projection_matrix,
    output_projection_matrix,
    adapter_down_matrix,
    adapter_up_matrix,
    adapter_choice_index,
    lengths,
    rotated_key_cache,
    cached_value_rows,
):
    requests = hidden_state_input.shape[0]
    width_part = hidden_state_input.shape[1]
    cached = rotated_key_cache.shape[1]
    kv_local = rotated_key_cache.shape[2]
    head_dim = rotated_key_cache.shape[3]
    query_cols = query_projection_matrix.shape[1]
    heads_local = query_cols // head_dim
    group_size = heads_local // kv_local
    seq_index = lax.axis_index(SEQ)
    head_index = lax.axis_index(HEAD)
    model_width = width_part * lax.axis_size(SEQ)
    values32 = hidden_state_input.astype(jnp.float32)
    square_part = jnp.sum(values32 * values32, axis=1)
    scaled = (values32 * attention_norm_gain.astype(jnp.float32)[None, :]).astype(jnp.bfloat16)
    query_part = jnp.dot(scaled, query_projection_matrix, preferred_element_type=jnp.float32)
    key_part = jnp.dot(scaled, key_projection_matrix, preferred_element_type=jnp.float32)
    value_part = jnp.dot(scaled, value_projection_matrix, preferred_element_type=jnp.float32)
    down_row_count = adapter_down_matrix.shape[0]
    resident_down_map = adapter_choice_index - head_index * down_row_count
    down_owned = (resident_down_map >= 0) & (resident_down_map < down_row_count)
    down_map_rows = adapter_down_matrix[jnp.clip(resident_down_map, 0, down_row_count - 1)]
    down_part = jnp.einsum("by,bey->be", scaled, down_map_rows, preferred_element_type=jnp.float32)
    down_part = jnp.where(down_owned[:, None], down_part, 0.0)
    own_square = jnp.where(head_index == 0, square_part, 0.0)
    down_total_sum, square_sum = in_one(
        (down_part, own_square), (("seq_0", "seq_1"), ("head_0", "head_1"))
    )
    inverse_factor = lax.rsqrt(square_sum / model_width + norm_epsilon)
    reduced_rank_state = (down_total_sum * inverse_factor[:, None] * adapter_scale_factor).astype(
        jnp.bfloat16
    )
    up_row_count = adapter_up_matrix.shape[0]
    resident_up_map = adapter_choice_index - seq_index * up_row_count
    up_owned = (resident_up_map >= 0) & (resident_up_map < up_row_count)
    up_map_rows = adapter_up_matrix[jnp.clip(resident_up_map, 0, up_row_count - 1)]
    expand = jnp.einsum(
        "rk,rkc->rc", reduced_rank_state, up_map_rows, preferred_element_type=jnp.float32
    )
    expand = jnp.where(up_owned[:, None], expand, 0.0)
    query_full, key_new, value_new = in_one_2(
        (
            query_part * inverse_factor[:, None] + expand,
            key_part * inverse_factor[:, None],
            value_part * inverse_factor[:, None],
        ),
        SEQ,
    )
    query_rot = rotate(query_full.reshape(requests, heads_local, head_dim), lengths).astype(
        jnp.bfloat16
    )
    key_rot = rotate(key_new.reshape(requests, kv_local, head_dim), lengths).astype(jnp.bfloat16)
    value_own = value_new.reshape(requests, kv_local, head_dim).astype(jnp.bfloat16)
    grouped = query_rot.reshape(requests, kv_local, group_size, head_dim)
    score_scale = head_dim ** (-0.5)
    scores = (
        jnp.einsum(
            "rhgd,rjhd->rhgj", grouped, rotated_key_cache, preferred_element_type=jnp.float32
        )
        * score_scale
    )
    position = seq_index * cached + jnp.arange(cached, dtype=jnp.int32)
    valid_mask = (position[None, :] < lengths[:, None])[:, None, None, :]
    scores = jnp.where(valid_mask, scores, masked_score)
    local_max = jnp.max(scores, axis=-1)
    weights = jnp.where(valid_mask, jnp.exp(scores - local_max[..., None]), 0.0)
    local_total = jnp.sum(weights, axis=-1)
    local_out = jnp.einsum(
        "rhgj,rjhd->rhgd",
        weights.astype(jnp.bfloat16),
        cached_value_rows,
        preferred_element_type=jnp.float32,
    )
    own_score = (
        jnp.einsum("rhgd,rhd->rhg", grouped, key_rot, preferred_element_type=jnp.float32)
        * score_scale
    )
    own_value = value_own.astype(jnp.float32)[:, :, None, :]
    whole_max, total_sum, out_sum = merged_by_axis(
        (local_max, local_total, local_out), SEQ, combine_parts
    )
    overall = jnp.maximum(whole_max, own_score)
    factor = jnp.exp(whole_max - overall)
    own_weight = jnp.exp(own_score - overall)
    denominator = total_sum * factor + own_weight
    summed = out_sum * factor[..., None] + own_weight[..., None] * own_value
    attended = (summed / denominator[..., None]).reshape(requests, query_cols).astype(jnp.bfloat16)
    out_part = jnp.dot(attended, output_projection_matrix, preferred_element_type=jnp.float32)
    output_sum = taken_together(out_part, HEAD)
    return output_sum.astype(jnp.bfloat16)


def solution(mesh):
    finer = Mesh(mesh.devices.reshape(16, 4, 4, 2), ("seq_0", "seq_1", "head_0", "head_1"))
    placed = (
        P(None, SEQ),
        P(SEQ),
        P(SEQ, HEAD),
        P(SEQ, HEAD),
        P(SEQ, HEAD),
        P(HEAD, SEQ),
        P(HEAD, None, SEQ),
        P(SEQ, None, HEAD),
        P(),
        P(),
        P(None, SEQ, HEAD, None),
        P(None, SEQ, HEAD, None),
    )
    return jax.shard_map(body, mesh=finer, in_specs=placed, out_specs=P(None, SEQ), check_vma=False)
```

profile of v0, /device:TPU:1, one launch (start us, length us, event | category | flops | bytes accessed | tf_op | source)
XLA Modules:
  0.0 151.1 jit_solution(3794468762930118020)
XLA Ops:
  0.0 0.7 copy-done.6
  0.8 0.6 copy-done.10
  1.4 1.5 %gather_fusion = bf16[16,16,128]{2,1,0:T(8,128)(2,1)S(1)} fusion(bf16[64,16,128]{2,1,0:T(8,128)(2,1)} %param.18, s32[1024]{0:T(1024)S(1)} %pad_clamp_fusion.1), kind=kCustom, calls=%fused_computation | custom fusion | bytes 131136 | tf_op jit(solution)/shard_map/gather | solution.py:183
  3.4 13.8 %all_to_all.32 = f32[8,1,272]{2,1,0:T(1,128)S(1)} all-to-all(f32[8,1,272]{2,1,0:T(1,128)S(1)} %broadcast_in_dim.63), channel_id=1, replica_groups=mesh['seq_0'=16,'seq_1'=4,'head_0'=4,'head_1'=2] {'head_0','head_1'}, dimensions={0} | all-to-all | bytes 17408 | tf_op jit(solution)/shard_map/all_to_all | solution.py:19
  17.3 0.7 broadcast_in_dim.64
  18.0 15.0 %all-to-all-start.1 = ((f32[64,1,272]{2,1,0:T(1,128)}), f32[64,1,272]{2,1,0:T(1,128)S(1)}, u32[]{:S(2)}, u32[]{:S(2)}) async-start(f32[64,1,272]{2,1,0:T(1,128)} %broadcast_in_dim.64), calls=%async_computation.1 | async-start | bytes 196608 | tf_op jit(solution)/shard_map/all_to_all | solution.py:19
  33.0 0.6 gather_fusion.1
  33.6 14.0 %all-to-all-done.1 = f32[64,1,272]{2,1,0:T(1,128)S(1)} async-done(((f32[64,1,272]{2,1,0:T(1,128)}), f32[64,1,272]{2,1,0:T(1,128)S(1)}, u32[]{:S(2)}, u32[]{:S(2)}) %all-to-all-start.1) | async-done | bytes 69664 | tf_op jit(solution)/shard_map/all_to_all | solution.py:19
  47.9 0.2 fusion.62
  48.1 0.7 copy-done.4
  49.0 0.7 copy-done.8
  49.9 0.7 copy-done.9
  50.7 0.8 all_to_all.23
  51.4 5.3 %all-to-all-start.2 = ((f32[64,1,320]{2,1,0:T(1,128)}), f32[64,1,320]{2,1,0:T(1,128)S(1)}, u32[]{:S(2)}, u32[]{:S(2)}) async-start(f32[64,1,320]{2,1,0:T(1,128)} %all_to_all.23), calls=%async_computation.2 | async-start | bytes 196608 | tf_op jit(solution)/shard_map/all_to_all | solution.py:48
  56.8 14.4 %all-to-all-done.2 = f32[64,1,320]{2,1,0:T(1,128)S(1)} async-done(((f32[64,1,320]{2,1,0:T(1,128)}), f32[64,1,320]{2,1,0:T(1,128)S(1)}, u32[]{:S(2)}, u32[]{:S(2)}) %all-to-all-start.2) | async-done | bytes 81952 | tf_op jit(solution)/shard_map/all_to_all | solution.py:48
  71.3 0.7 broadcast_in_dim.68
  72.0 4.6 %all-to-all-start.3 = ((f32[64,1,320]{2,1,0:T(1,128)}), f32[64,1,320]{2,1,0:T(1,128)S(1)}, u32[]{:S(2)}, u32[]{:S(2)}) async-start(f32[64,1,320]{2,1,0:T(1,128)} %broadcast_in_dim.68), calls=%async_computation.3 | async-start | bytes 196608 | tf_op jit(solution)/shard_map/all_to_all | solution.py:19
  76.8 14.4 %all-to-all-done.3 = f32[64,1,320]{2,1,0:T(1,128)S(1)} async-done(((f32[64,1,320]{2,1,0:T(1,128)}), f32[64,1,320]{2,1,0:T(1,128)S(1)}, u32[]{:S(2)}, u32[]{:S(2)}) %all-to-all-start.3) | async-done | bytes 81952 | tf_op jit(solution)/shard_map/all_to_all | solution.py:19
  91.1 0.2 reduce.7
  91.7 0.5 fusion.184
  92.2 0.2 fusion.8
  92.4 0.2 copy-done.1
  92.6 0.3 fusion.3
  93.1 23.5 %all-gather.2 = bf16[16,130,128]{2,1,0:T(8,128)(2,1)S(1)} all-gather(bf16[1,130,128]{2,1,0:T(8,128)(2,1)S(1)} %maximum_bitcast_fusion), channel_id=2, replica_groups=mesh['seq_0'=16,'seq_1'=4,'head_0'=4,'head_1'=2] {'seq_0'}, dimensions={0}, use_global_device_ids=true | all-gather | bytes 565760 | tf_op jit(solution)/shard_map/all_gather | solution.py:91
  116.8 0.6 fusion.16
  117.4 9.4 %all-gather.3 = bf16[4,130,128]{2,1,0:T(8,128)(2,1)S(1)} all-gather(bf16[1,130,128]{2,1,0:T(8,128)(2,1)S(1)} %maximum_bitcast_fusion.1), channel_id=3, replica_groups=mesh['seq_0'=16,'seq_1'=4,'head_0'=4,'head_1'=2] {'seq_1'}, dimensions={0}, use_global_device_ids=true | all-gather | bytes 166400 | tf_op jit(solution)/shard_map/all_gather | solution.py:91
  127.1 0.2 fusion.66
  128.0 0.3 convert_reduce_fusion
  129.3 0.4 copy-done.3
  129.7 0.2 fusion.48
  129.9 20.6 %all_to_all.33 = f32[8,16,128]{2,1,0:T(8,128)S(1)} all-to-all(f32[8,16,128]{2,1,0:T(8,128)S(1)} %broadcast_in_dim.71), channel_id=1, replica_groups=mesh['seq_0'=16,'seq_1'=4,'head_0'=4,'head_1'=2] {'head_0','head_1'}, dimensions={0} | all-to-all | bytes 131072 | tf_op jit(solution)/shard_map/all_to_all | solution.py:19
  150.5 0.6 reduce_sum.59
  (91 shorter events, 4.0 us)
Async XLA Ops:
  0.0 91.7 %copy-start = (bf16[16,256,1,128]{3,1,2,0:T(8,128)(2,1)S(1)}, bf16[16,256,1,128]{3,1,2,0:T(8,128)(2,1)}, u32[]{:S(2)}) copy-start(bf16[16,256,1,128]{3,1,2,0:T(8,128)(2,1)} %param.22) | copy-start | bytes 3145732
  0.0 0.7 copy-start.6
  0.8 0.7 copy-start.10
  1.4 1.5 %copy-start.5 = (bf16[16,128]{1,0:T(8,128)(2,1)S(1)}, bf16[16,128]{1,0:T(8,128)(2,1)}, u32[]{:S(2)}) copy-start(bf16[16,128]{1,0:T(8,128)(2,1)} %param.12) | copy-start | bytes 12292
  3.0 30.0 %copy-start.2 = (bf16[8,16,1024]{2,1,0:T(8,128)(2,1)S(1)}, bf16[8,16,1024]{2,1,0:T(8,128)(2,1)}, u32[]{:S(2)}) copy-start(bf16[8,16,1024]{2,1,0:T(8,128)(2,1)} %param.19) | copy-start | bytes 786436
  18.0 15.0 %copy-start.7 = (s32[16]{0:T(128)S(1)}, s32[16]{0:T(128)}, u32[]{:S(2)}) copy-start(s32[16]{0:T(128)} %param.21) | copy-start | bytes 196
  18.0 29.6 %all-to-all-start.1 = ((f32[64,1,272]{2,1,0:T(1,128)}), f32[64,1,272]{2,1,0:T(1,128)S(1)}, u32[]{:S(2)}, u32[]{:S(2)}) async-start(f32[64,1,272]{2,1,0:T(1,128)} %broadcast_in_dim.64), calls=%async_computation.1 | async-start | bytes 196608 | tf_op jit(solution)/shard_map/all_to_all | solution.py:19
  47.9 1.0 copy-start.4
  49.0 0.8 copy-start.8
  49.8 0.8 copy-start.9
  51.4 19.8 %all-to-all-start.2 = ((f32[64,1,320]{2,1,0:T(1,128)}), f32[64,1,320]{2,1,0:T(1,128)S(1)}, u32[]{:S(2)}, u32[]{:S(2)}) async-start(f32[64,1,320]{2,1,0:T(1,128)} %all_to_all.23), calls=%async_computation.2 | async-start | bytes 196608 | tf_op jit(solution)/shard_map/all_to_all | solution.py:48
  72.0 19.1 %all-to-all-start.3 = ((f32[64,1,320]{2,1,0:T(1,128)}), f32[64,1,320]{2,1,0:T(1,128)S(1)}, u32[]{:S(2)}, u32[]{:S(2)}) async-start(f32[64,1,320]{2,1,0:T(1,128)} %broadcast_in_dim.68), calls=%async_computation.3 | async-start | bytes 196608 | tf_op jit(solution)/shard_map/all_to_all | solution.py:19
  91.4 1.2 copy-start.1
  128.7 1.0 copy-start.3
where the time goes:
time: 152 us; the launch traced here: 151 us
  blocking collectives  67.3 us (44%)
  waiting for transfers between devices  42.8 us (28%)
  starting transfers between devices  24.9 us (16%)
  local copies, waits for them, and re-layouts  10.5 us (7%)
  other arithmetic  3.31 us (2%)
  matrix products  1.87 us (1%)
    all_to_all x2, blocking collectives, sent_to_all(): return lax.all_to_all(copies, axis, split_axis=0, concat_axis=0, tiled=True)  34.4 us
    all_gather x2, blocking collectives, all_in_one(): both, at, found = (lax.all_gather(jnp.concatenate(lines), axis), 0, {})  32.9 us
    all_to_all x2, waiting for transfers between devices, sent_to_all(): return lax.all_to_all(copies, axis, split_axis=0, concat_axis=0, tiled=True)  28.4 us
    all_to_all x2, starting transfers between devices, sent_to_all(): return lax.all_to_all(copies, axis, split_axis=0, concat_axis=0, tiled=True)  19.6 us
    all_to_all x1, waiting for transfers between devices, sum_at_owner(): lax.all_to_all(pieces, axis, split_axis=0, concat_axis=0, tiled=True)  14.4 us
    all_to_all x1, starting transfers between devices, sum_at_owner(): lax.all_to_all(pieces, axis, split_axis=0, concat_axis=0, tiled=True)  5.28 us
    unnamed x23, local copies, waits for them, and re-layouts  4.17 us
  transfers between devices with their start and end apart: 3, of which 3 were waited for; matrix products, arithmetic and copies ran while one was open for 1% of the time, Pallas kernels for 0%

commit v1 on v0

v1 whole, which is shorter than its diff:
```python
import jax
import jax.numpy as jnp
from jax import lax
from jax.experimental import pallas as pl
from jax.experimental.pallas import tpu as pltpu
from jax.sharding import PartitionSpec as P

MESH = pl.DeviceIdType.MESH
F32 = jnp.float32
BF16 = jnp.bfloat16

norm_epsilon = 1e-05
rope_base = 500000.0
masked_score = -1e30

NY, NZ, NH = 4, 16, 8
PLANE = [(dy, dh) for dy in range(NY) for dh in range(NH) if (dy, dh) != (0, 0)]
COLUMN = list(range(1, NZ))
WINDOW = [(dy, dz) for dz in (2, -1, 1, 0) for dy in (2, 1, 3, 0) if (dy, dz) != (0, 0)]
QUARTER = [8, 4, 12]
HEADS = list(range(1, NH))
STAGES = 11


def kernel(
    hid_h, gain_h, wq_h, wk_h, wv_h, wo_h, down_h, up_h, choice, lengths, kc_h, vc_h,
    out,
    hid, gain, wq, wk, wv, wo, down, up, kc, vc,
    t1a, t1b, rsb_src, rsb, z2b, rse_src, rse, z2e, agq, rso_src, rso, z2o, ago, hbuf,
    load_sem, send_sem, recv_sem,
):
    seq = lax.axis_index("seq")
    head = lax.axis_index("head")
    y = lax.rem(seq, NY)
    z = lax.div(seq, NY)
    mine = y * 4 + lax.rem(z, 4)

    def at(dy, dz, dh):
        yy = lax.rem(y + (dy + NY) % NY, NY)
        zz = lax.rem(z + (dz + NZ) % NZ, NZ)
        return (zz * NY + yy, lax.rem(head + (dh + NH) % NH, NH))

    barrier = pltpu.get_barrier_semaphore()
    greeted = [(0, dz, 0) for dz in COLUMN]
    greeted += [(-dy, -dz, 0) for dy, dz in WINDOW if dy and dz]
    greeted += [(dy, 0, dh) for dy, dh in PLANE]
    for dy, dz, dh in greeted:
        pl.semaphore_signal(barrier, inc=1, device_id=at(dy, dz, dh), device_id_type=MESH)

    loads = [
        pltpu.make_async_copy(src, dst, load_sem.at[k])
        for k, (src, dst) in enumerate(
            [(hid_h, hid), (gain_h, gain), (down_h, down), (wq_h, wq), (wk_h, wk), (wv_h, wv),
             (up_h, up), (kc_h, kc), (vc_h, vc), (wo_h, wo)]
        )
    ]
    for c in loads:
        c.start()

    def send(stage, src, dst, where):
        pltpu.make_async_remote_copy(
            src_ref=src, dst_ref=dst, send_sem=send_sem.at[stage], recv_sem=recv_sem.at[stage],
            device_id=at(*where), device_id_type=MESH,
        ).start()

    def bundle(stage, view):
        return pltpu.make_async_remote_copy(
            src_ref=view, dst_ref=view, send_sem=send_sem.at[stage], recv_sem=recv_sem.at[stage],
            device_id=at(0, 1, 0), device_id_type=MESH,
        )

    rows = lax.broadcasted_iota(jnp.int32, (16, 128), 0)
    lane = lax.broadcasted_iota(jnp.int32, (16, 128), 1)
    group = lane // 16
    rows8 = lax.rem(rows, 8)
    lane8 = lax.broadcasted_iota(jnp.int32, (8, 128), 1)
    chosen = jnp.zeros((16, 128), jnp.int32)
    for r in range(16):
        chosen = jnp.where(rows == r, choice[r], chosen)

    for c in loads[:3]:
        c.wait()
    values = hid[...].astype(F32)
    scaled = (values * gain[...].astype(F32)).astype(BF16)
    every = lax.dot_general(
        scaled, down[...], (((1,), (1,)), ((), ())), preferred_element_type=F32
    )
    fold = jnp.zeros((16, 128), F32)
    for j in range(8):
        fold += jnp.where(
            chosen == head * 64 + j * 8 + group, every[:, j * 128 : (j + 1) * 128], 0.0
        )
    for shift in (64, 32, 16):
        fold += pltpu.roll(fold, shift, 1)
    diagonal = jnp.where(group == rows8, fold, 0.0)
    square = jnp.sum(values * values, axis=1, keepdims=True)
    t1a[0, 0:1, :] = jnp.sum(diagonal[0:8], axis=0, keepdims=True)
    t1a[0, 1:2, :] = jnp.sum(diagonal[8:16], axis=0, keepdims=True)
    t1a[0, 2:3, :] = jnp.sum(jnp.where(lane == rows, square, 0.0), axis=0, keepdims=True)
    t1a[0, 3:4, :] = jnp.zeros((1, 128), F32)

    pl.semaphore_wait(barrier, len(greeted))
    for k, (dy, dh) in enumerate(PLANE):
        send(0, t1a.at[0], t1a.at[k + 1], (dy, 0, dh))

    for c in loads[3:6]:
        c.wait()
    query_part = jnp.dot(scaled, wq[...], preferred_element_type=F32)
    key_part = jnp.dot(scaled, wk[...], preferred_element_type=F32)
    value_part = jnp.dot(scaled, wv[...], preferred_element_type=F32)
    for j in range(8):
        rsb_src[pl.ds(j, 16, stride=16), :] = query_part[:, j * 128 : (j + 1) * 128]
    rsb_src[pl.ds(8, 16, stride=16), :] = key_part
    rsb_src[pl.ds(9, 16, stride=16), :] = value_part
    for j in range(10, 16):
        rsb_src[pl.ds(j, 16, stride=16), :] = jnp.zeros((16, 128), F32)

    def row_of(dy, dz):
        return lax.rem(y + dy, 4) * 4 + lax.rem(lax.rem(z, 4) + dz + 4, 4)

    def rows_at(r, n):
        return pl.ds(pl.multiple_of(r * n, n), n)

    for k, (dy, dz) in enumerate(WINDOW):
        send(2, rsb_src.at[rows_at(row_of(dy, dz), 16)], rsb.at[k], (dy, dz, 0))

    bundle(0, t1a.at[1:32]).wait_recv()
    t1b[0] = jnp.sum(t1a[...], axis=0)
    for k, dz in enumerate(COLUMN):
        send(1, t1b.at[0], t1b.at[k + 1], (0, dz, 0))

    bundle(2, rsb).wait_recv()
    base = rsb_src[rows_at(mine, 16), :]
    for k in range(15):
        base += rsb[k]
    z2b[0] = base
    for k, dz in enumerate(QUARTER):
        send(3, z2b.at[0], z2b.at[k + 1], (0, dz, 0))

    bundle(1, t1b.at[1:16]).wait_recv()
    whole = jnp.sum(t1b[...], axis=0)
    spread = jnp.concatenate(
        [jnp.broadcast_to(whole[0:1], (8, 128)), jnp.broadcast_to(whole[1:2], (8, 128))], axis=0
    )
    spread = jnp.where(group == rows8, spread, 0.0)
    for shift in (64, 32, 16):
        spread += pltpu.roll(spread, shift, 1)
    squares = jnp.sum(
        jnp.where(lane == rows, jnp.broadcast_to(whole[2:3], (16, 128)), 0.0),
        axis=1,
        keepdims=True,
    )
    inverse = lax.rsqrt(squares * (1.0 / (NH * 8192.0)) + norm_epsilon)
    shrunk = (spread * inverse).astype(BF16).astype(F32)
    placed = jnp.where(chosen == seq * 8 + group, shrunk, 0.0).astype(BF16)
    loads[6].wait()
    expand = jnp.dot(placed, up[...], preferred_element_type=F32)
    for j in range(8):
        rse_src[pl.ds(j, 16, stride=8), :] = expand[:, j * 128 : (j + 1) * 128]
    for k, (dy, dz) in enumerate(WINDOW):
        send(4, rse_src.at[rows_at(row_of(dy, dz), 8)], rse.at[k], (dy, dz, 0))

    inverse_mine = jnp.sum(jnp.where(rows == mine, inverse, 0.0), axis=0, keepdims=True)
    half = lax.rem(lane8, 64).astype(F32)
    frequency = jnp.exp(-half * (jnp.log(jnp.full((8, 128), rope_base, F32)) / 64.0))
    angle = lengths[mine].astype(F32) * frequency
    cosine = jnp.cos(angle)
    sine = jnp.where(lane8 < 64, -jnp.sin(angle), jnp.sin(angle))

    bundle(3, z2b.at[1:4]).wait_recv()
    base = (z2b[0] + z2b[1]) + (z2b[2] + z2b[3])
    base = base * inverse_mine
    bundle(4, rse).wait_recv()
    grown = rse_src[rows_at(mine, 8), :]
    for k in range(15):
        grown += rse[k]
    z2e[0] = grown
    for k, dz in enumerate(QUARTER):
        send(5, z2e.at[0], z2e.at[k + 1], (0, dz, 0))

    def rotated(x):
        return (x * cosine + pltpu.roll(x, 64, 1) * sine).astype(BF16)

    key_rot = rotated(jnp.broadcast_to(base[8:9], (8, 128))).astype(F32)
    value_own = jnp.broadcast_to(base[9:10], (8, 128)).astype(BF16).astype(F32)
    bundle(5, z2e.at[1:4]).wait_recv()
    query = base[0:8] + ((z2e[0] + z2e[1]) + (z2e[2] + z2e[3]))
    query_rot = rotated(query)
    agq[mine] = query_rot
    for dy, dz in WINDOW:
        send(6, agq.at[mine], agq.at[mine], (dy, dz, 0))
    scale = 128.0**-0.5
    own_score = jnp.sum(query_rot.astype(F32) * key_rot, axis=1, keepdims=True) * scale

    loads[7].wait()
    loads[8].wait()
    bundle(6, agq.at[0:15]).wait_recv()
    position = lax.broadcasted_iota(jnp.int32, (8, 256), 1) + seq * 256
    for r in range(16):
        scores = (
            lax.dot_general(agq[r], kc[r], (((1,), (1,)), ((), ())), preferred_element_type=F32)
            * scale
        )
        valid = position < lengths[r]
        scores = jnp.where(valid, scores, masked_score)
        top = jnp.max(scores, axis=1, keepdims=True)
        weights = jnp.where(valid, jnp.exp(scores - top), 0.0)
        total = jnp.sum(weights, axis=1, keepdims=True)
        rso_src[r, 0:8, :] = jnp.dot(weights.astype(BF16), vc[r], preferred_element_type=F32)
        rso_src[r, 8:16, :] = jnp.where(lane8 < 64, top, total)
    for k, (dy, dz) in enumerate(WINDOW):
        send(7, rso_src.at[row_of(dy, dz)], rso.at[k], (dy, dz, 0))

    def merged(parts):
        tops, totals, outs = [], [], []
        for part in parts:
            stat = part[8:16]
            swapped = pltpu.roll(stat, 64, 1)
            tops.append(jnp.where(lane8 < 64, stat, swapped))
            totals.append(jnp.where(lane8 < 64, swapped, stat))
            outs.append(part[0:8])
        top = tops[0]
        for t in tops[1:]:
            top = jnp.maximum(top, t)
        total = jnp.zeros((8, 128), F32)
        result = jnp.zeros((8, 128), F32)
        for t, s, o in zip(tops, totals, outs):
            factor = jnp.exp(t - top)
            total += s * factor
            result += o * factor
        return top, total, result

    bundle(7, rso).wait_recv()
    top, total, result = merged([rso_src[mine]] + [rso[k] for k in range(15)])
    z2o[0, 0:8, :] = result
    z2o[0, 8:16, :] = jnp.where(lane8 < 64, top, total)
    for k, dz in enumerate(QUARTER):
        send(8, z2o.at[0], z2o.at[k + 1], (0, dz, 0))
    bundle(8, z2o.at[1:4]).wait_recv()
    top, total, result = merged([z2o[k] for k in range(4)])
    peak = jnp.maximum(top, own_score)
    factor = jnp.exp(top - peak)
    own_weight = jnp.exp(own_score - peak)
    attended = (result * factor + own_weight * value_own) / (total * factor + own_weight)
    ago[rows_at(mine, 8), :] = attended.astype(BF16).astype(F32)
    for dy, dz in WINDOW:
        send(9, ago.at[rows_at(mine, 8)], ago.at[rows_at(mine, 8)], (dy, dz, 0))

    loads[9].wait()
    bundle(9, ago.at[0:120]).wait_recv()
    projected = jnp.zeros((16, 128), F32)
    for j in range(8):
        projected += jnp.dot(
            ago[pl.ds(j, 16, stride=8), :].astype(BF16),
            wo[j * 128 : (j + 1) * 128, :],
            preferred_element_type=F32,
        )
    hbuf[0] = projected
    for k, dh in enumerate(HEADS):
        send(10, hbuf.at[0], hbuf.at[k + 1], (0, 0, dh))
    bundle(10, hbuf.at[1:8]).wait_recv()
    out[...] = jnp.sum(hbuf[...], axis=0).astype(BF16)

    for stage, view in enumerate(
        [t1a.at[1:32], t1b.at[1:16], rsb, z2b.at[1:4], rse, z2e.at[1:4], agq.at[0:15], rso,
         z2o.at[1:4], ago.at[0:120], hbuf.at[1:8]]
    ):
        bundle(stage, view).wait_send()


def body(hid, gain, wq, wk, wv, wo, down, up, choice, lengths, kc, vc):
    anywhere = pl.BlockSpec(memory_space=pl.ANY)
    scalars = pl.BlockSpec(memory_space=pltpu.SMEM)
    return pl.pallas_call(
        kernel,
        out_shape=jax.ShapeDtypeStruct((16, 128), BF16),
        in_specs=[anywhere] * 8 + [scalars] * 2 + [anywhere] * 2,
        out_specs=pl.BlockSpec(memory_space=pltpu.VMEM),
        scratch_shapes=[
            pltpu.VMEM((16, 128), BF16),
            pltpu.VMEM((1, 128), BF16),
            pltpu.VMEM((128, 1024), BF16),
            pltpu.VMEM((128, 128), BF16),
            pltpu.VMEM((128, 128), BF16),
            pltpu.VMEM((1024, 128), BF16),
            pltpu.VMEM((1024, 128), BF16),
            pltpu.VMEM((128, 1024), BF16),
            pltpu.VMEM((16, 256, 128), BF16),
            pltpu.VMEM((16, 256, 128), BF16),
            pltpu.VMEM((32, 4, 128), F32),
            pltpu.VMEM((16, 4, 128), F32),
            pltpu.VMEM((256, 128), F32),
            pltpu.VMEM((15, 16, 128), F32),
            pltpu.VMEM((4, 16, 128), F32),
            pltpu.VMEM((128, 128), F32),
            pltpu.VMEM((15, 8, 128), F32),
            pltpu.VMEM((4, 8, 128), F32),
            pltpu.VMEM((16, 8, 128), BF16),
            pltpu.VMEM((16, 16, 128), F32),
            pltpu.VMEM((15, 16, 128), F32),
            pltpu.VMEM((4, 16, 128), F32),
            pltpu.VMEM((128, 128), F32),
            pltpu.VMEM((8, 16, 128), F32),
            pltpu.SemaphoreType.DMA((10,)),
            pltpu.SemaphoreType.DMA((STAGES,)),
            pltpu.SemaphoreType.DMA((STAGES,)),
        ],
        compiler_params=pltpu.CompilerParams(collective_id=0, has_side_effects=True),
    )(
        hid, gain.reshape(1, 128), wq, wk, wv, wo, down.reshape(1024, 128), up.reshape(128, 1024),
        choice, lengths, kc.reshape(16, 256, 128), vc.reshape(16, 256, 128),
    )


def solution(mesh):
    placed = (
        P(None, "seq"),
        P("seq"),
        P("seq", "head"),
        P("seq", "head"),
        P("seq", "head"),
        P("head", "seq"),
        P("head", None, "seq"),
        P("seq", None, "head"),
        P(),
        P(),
        P(None, "seq", "head", None),
        P(None, "seq", "head", None),
    )
    return jax.shard_map(
        body, mesh=mesh, in_specs=placed, out_specs=P(None, "seq"), check_vma=False
    )
```

time: 152 us -> 75.3 us (0.50)
  Pallas kernels: 0 us -> 73.9 us
  blocking collectives: 67.3 us -> 0 us
  waiting for transfers between devices: 42.8 us -> 0 us
  starting transfers between devices: 24.9 us -> 0 us
  local copies, waits for them, and re-layouts: 10.5 us -> 1.28 us
  other arithmetic: 3.31 us -> 0 us
  matrix products: 1.87 us -> 0 us
    pallas_call x0 -> x1, Pallas kernels: none -> 73.9 us  [body(): pl.pallas_call(kernel, out_shape=jax.ShapeDtypeStruct((16, 128), BF16), i...]
    all_to_all x3 -> x0, waiting for transfers between devices: 42.8 us -> none  [the longest x2 28.4 us: sent_to_all(): return lax.all_to_all(copies, axis, split_axis=0, concat_axis=0, tiled=True)]
    all_to_all x2 -> x0, blocking collectives: 34.4 us -> none  [sent_to_all(): return lax.all_to_all(copies, axis, split_axis=0, concat_axis=0, tiled=True)]
    all_gather x2 -> x0, blocking collectives: 32.9 us -> none  [all_in_one(): both, at, found = (lax.all_gather(jnp.concatenate(lines), axis), 0, {})]
    all_to_all x3 -> x0, starting transfers between devices: 24.9 us -> none  [the longest x2 19.6 us: sent_to_all(): return lax.all_to_all(copies, axis, split_axis=0, concat_axis=0, tiled=True)]
    unnamed x23 -> x1, local copies, waits for them, and re-layouts: 4.17 us -> 1.28 us
    gather x2 -> x0, local copies, waits for them, and re-layouts: 2.12 us -> none  [the longest x1 1.54 us: body(): adapter_down_matrix[jnp.clip(resident_down_map, 0, down_row_count - 1)]]
    dot_general x9 -> x0, matrix products: 1.87 us -> none  [the longest x1 0.49 us: body(): jnp.einsum('rhgd,rjhd->rhgj', grouped, rotated_key_cache, preferred_eleme...]
  transfers between devices with their start and end apart: 3 -> 0, of which waited for: 3 -> 0; matrix products, arithmetic and copies ran while one was open for 1% -> 0% of each run, Pallas kernels for 0% -> 0%
where the time goes in v1:
time: 75.3 us; the launch traced here: 75.1 us
  Pallas kernels  73.9 us (98%)
  local copies, waits for them, and re-layouts  1.28 us (2%)
    pallas_call x1, Pallas kernels, body(): pl.pallas_call(kernel, out_shape=jax.ShapeDtypeStruct((16, 128), BF16), i...  73.9 us

profile of v1, /device:TPU:1, one launch (start us, length us, event | category | flops | bytes accessed | tf_op | source)
XLA Modules:
  0.0 75.1 jit_solution(7433519047693511323)
XLA Ops:
  0.0 73.9 %shard_map.118 = bf16[16,128]{1,0:T(8,128)(2,1)} custom-call(bf16[16,128]{1,0:T(8,128)(2,1)} %hid_h.1, bf16[1,128]{1,0:T(2,128)(2,1)} %bitcast.9, bf16[128,1024]{1,0:T(8,128)(2,1)} %wq_h.1, bf16[128,128]{1,0:T(8,128)(2,1)} %wk_h.1, bf16[128,128]{1,0:T(8,128)(2,1)} %wv_h.1, bf16[1024,128]{1,0:T(8,128)(2,1)} %wo_h.1, bf16[1024,128]{1,0:T(8,128)(2,1)} %bitcast.7, ...), custom_call_target="tpu_custom_call" | custom-call | tf_op jit(solution)/shard_map/pallas_call | solution.py:274
  73.9 1.3 %copy.14 = bf16[16,128]{1,0:T(8,128)(2,1)} copy(bf16[16,128]{1,0:T(8,128)(2,1)} %shard_map.118) | data formatting | bytes 8192

commit v2 on v1

v2 whole, which is shorter than its diff:
```python
import jax
import jax.numpy as jnp
from jax import lax
from jax.experimental import pallas as pl
from jax.experimental.pallas import tpu as pltpu
from jax.sharding import PartitionSpec as P

MESH = pl.DeviceIdType.MESH
F32 = jnp.float32
BF16 = jnp.bfloat16

norm_epsilon = 1e-05
rope_base = 500000.0
masked_score = -1e30

NY, NZ, NH = 4, 16, 8
PLANE = [(dy, dh) for dy in range(NY) for dh in range(NH) if (dy, dh) != (0, 0)]
COLUMN = list(range(1, NZ))
WINDOW = [(dy, dz) for dz in (2, -1, 1, 0) for dy in (2, 1, 3, 0) if (dy, dz) != (0, 0)]
QUARTER = [8, 4, 12]
HEADS = list(range(1, NH))
NEAR = [1, -1, 2, -2, 3, -3, 4, -4]
STAGES = 11


def kernel(
    hid_h, gain_h, wq_h, wk_h, wv_h, wo_h, down_h, up_h, choice_h, lengths_h, kc_h, vc_h,
    out,
    hid, gain, wq, wk, wv, wo, down, up, kc, vc, choice, lengths,
    t1a, t1b, flat, rsb_src, rsb, z2b, rse_src, rse, z2e, agq, rso_src, rso, z2o, ago, hbuf,
    load_sem, send_sem, recv_sem, vouch,
):
    seq = lax.axis_index("seq")
    head = lax.axis_index("head")
    y = lax.rem(seq, NY)
    z = lax.div(seq, NY)
    mine = y * 4 + lax.rem(z, 4)

    def at(dy, dz, dh):
        yy = lax.rem(y + (dy + NY) % NY, NY)
        zz = lax.rem(z + (dz + NZ) % NZ, NZ)
        return (zz * NY + yy, lax.rem(head + (dh + NH) % NH, NH))

    barrier = pltpu.get_barrier_semaphore()
    greeted = [(0, dz, 0) for dz in NEAR]
    greeted += [(-dy, -dz, 0) for dy, dz in WINDOW if dy and dz]
    greeted += [(dy, 0, dh) for dy, dh in PLANE]
    for dy, dz, dh in greeted:
        pl.semaphore_signal(barrier, inc=1, device_id=at(dy, dz, dh), device_id_type=MESH)

    loads = [
        pltpu.make_async_copy(src, dst, load_sem.at[k])
        for k, (src, dst) in enumerate(
            [(hid_h, hid), (gain_h, gain), (down_h, down), (wq_h, wq), (wk_h, wk), (wv_h, wv),
             (up_h, up), (kc_h, kc), (vc_h, vc), (wo_h, wo), (choice_h, choice),
             (lengths_h, lengths)]
        )
    ]
    for c in loads:
        c.start()

    def send(stage, src, dst, where):
        pltpu.make_async_remote_copy(
            src_ref=src, dst_ref=dst, send_sem=send_sem.at[stage], recv_sem=recv_sem.at[stage],
            device_id=at(*where), device_id_type=MESH,
        ).start()

    def bundle(stage, view):
        return pltpu.make_async_remote_copy(
            src_ref=view, dst_ref=view, send_sem=send_sem.at[stage], recv_sem=recv_sem.at[stage],
            device_id=at(0, 1, 0), device_id_type=MESH,
        )

    rows = lax.broadcasted_iota(jnp.int32, (16, 128), 0)
    lane = lax.broadcasted_iota(jnp.int32, (16, 128), 1)
    group = lane // 16
    rows8 = lax.rem(rows, 8)
    lane8 = lax.broadcasted_iota(jnp.int32, (8, 128), 1)
    loads[10].wait()
    chosen = jnp.zeros((16, 128), jnp.int32)
    for r in range(16):
        chosen = jnp.where(rows == r, choice[r], chosen)

    for c in loads[:3]:
        c.wait()
    values = hid[...].astype(F32)
    scaled = (values * gain[...].astype(F32)).astype(BF16)
    every = lax.dot_general(
        scaled, down[...], (((1,), (1,)), ((), ())), preferred_element_type=F32
    )
    fold = jnp.zeros((16, 128), F32)
    for j in range(8):
        fold += jnp.where(
            chosen == head * 64 + j * 8 + group, every[:, j * 128 : (j + 1) * 128], 0.0
        )
    for shift in (64, 32, 16):
        fold += pltpu.roll(fold, shift, 1)
    diagonal = jnp.where(group == rows8, fold, 0.0)
    square = jnp.sum(values * values, axis=1, keepdims=True)
    t1a[0, 0:1, :] = jnp.sum(diagonal[0:8], axis=0, keepdims=True)
    t1a[0, 1:2, :] = jnp.sum(diagonal[8:16], axis=0, keepdims=True)

    pl.semaphore_wait(barrier, len(greeted))
    for k, (dy, dh) in enumerate(PLANE):
        send(0, t1a.at[0], t1a.at[k + 1], (dy, 0, dh))
    for dz in (4, -4):
        pl.semaphore_signal(vouch, inc=1, device_id=at(0, dz, 0), device_id_type=MESH)

    for c in loads[3:6]:
        c.wait()
    query_part = jnp.dot(scaled, wq[...], preferred_element_type=F32)
    key_part = jnp.dot(scaled, wk[...], preferred_element_type=F32)
    value_part = jnp.dot(scaled, wv[...], preferred_element_type=F32)
    for j in range(8):
        flat[pl.ds(j, 16, stride=16), :] = query_part[:, j * 128 : (j + 1) * 128]
    flat[pl.ds(8, 16, stride=16), :] = key_part
    flat[pl.ds(9, 16, stride=16), :] = value_part
    flat[pl.ds(10, 16, stride=16), :] = jnp.broadcast_to(square, (16, 128))
    for j in range(11, 16):
        flat[pl.ds(j, 16, stride=16), :] = jnp.zeros((16, 128), F32)
    rsb_src[...] = flat[...].reshape(16, 16, 128).astype(BF16)

    def row_of(dy, dz):
        return lax.rem(y + dy, 4) * 4 + lax.rem(lax.rem(z, 4) + dz + 4, 4)

    for k, (dy, dz) in enumerate(WINDOW):
        send(2, rsb_src.at[row_of(dy, dz)], rsb.at[k], (dy, dz, 0))

    bundle(0, t1a.at[1:32]).wait_recv()
    t1b[0] = jnp.sum(t1a[...], axis=0)
    pl.semaphore_wait(vouch, 2)
    for k, dz in enumerate(COLUMN):
        send(1, t1b.at[0], t1b.at[k + 1], (0, dz, 0))

    bundle(2, rsb).wait_recv()
    base = rsb_src[mine].astype(F32)
    for k in range(15):
        base += rsb[k].astype(F32)
    z2b[0] = base.astype(BF16)
    for k, dz in enumerate(QUARTER):
        send(3, z2b.at[0], z2b.at[k + 1], (0, dz, 0))

    loads[11].wait()
    half = lax.rem(lane8, 64).astype(F32)
    frequency = jnp.exp(-half * (jnp.log(jnp.full((8, 128), rope_base, F32)) / 64.0))
    angle = lengths[mine].astype(F32) * frequency
    cosine = jnp.cos(angle)
    sine = jnp.sin(angle)
    sine = jnp.where(lane8 < 64, -sine, sine)

    loads[6].wait()
    bundle(1, t1b.at[1:16]).wait_recv()
    whole = jnp.sum(t1b[...], axis=0)
    spread = jnp.concatenate(
        [jnp.broadcast_to(whole[0:1], (8, 128)), jnp.broadcast_to(whole[1:2], (8, 128))], axis=0
    )
    spread = jnp.where(group == rows8, spread, 0.0)
    for shift in (64, 32, 16):
        spread += pltpu.roll(spread, shift, 1)
    placed = jnp.where(chosen == seq * 8 + group, spread, 0.0).astype(BF16)
    expand = jnp.dot(placed, up[...], preferred_element_type=F32)
    for j in range(8):
        flat[pl.ds(j, 16, stride=8), :] = expand[:, j * 128 : (j + 1) * 128]
    rse_src[...] = flat[0:128, :].reshape(16, 8, 128).astype(BF16)
    for k, (dy, dz) in enumerate(WINDOW):
        send(4, rse_src.at[row_of(dy, dz)], rse.at[k], (dy, dz, 0))

    bundle(3, z2b.at[1:4]).wait_recv()
    base = z2b[0].astype(F32)
    for k in range(1, 4):
        base += z2b[k].astype(F32)
    inverse = lax.rsqrt(base[10:11] * (1.0 / 8192.0) + norm_epsilon)
    bundle(4, rse).wait_recv()
    grown = rse_src[mine].astype(F32)
    for k in range(15):
        grown += rse[k].astype(F32)
    z2e[0] = grown.astype(BF16)
    for k, dz in enumerate(QUARTER):
        send(5, z2e.at[0], z2e.at[k + 1], (0, dz, 0))

    def rotated(x):
        return (x * cosine + pltpu.roll(x, 64, 1) * sine).astype(BF16)

    key_rot = rotated(jnp.broadcast_to(base[8:9] * inverse, (8, 128))).astype(F32)
    value_own = jnp.broadcast_to(base[9:10] * inverse, (8, 128)).astype(BF16).astype(F32)
    bundle(5, z2e.at[1:4]).wait_recv()
    query = base[0:8]
    for k in range(4):
        query += z2e[k].astype(F32)
    query_rot = rotated(query * inverse)
    agq[mine] = query_rot
    for dy, dz in WINDOW:
        send(6, agq.at[mine], agq.at[mine], (dy, dz, 0))
    scale = 128.0**-0.5
    own_score = jnp.sum(query_rot.astype(F32) * key_rot, axis=1, keepdims=True) * scale

    def packed(high, low, total, result):
        stat = jnp.where(lane8 < 32, high, jnp.where(lane8 < 64, low, total))
        return jnp.concatenate([result, stat], axis=0).astype(BF16)

    def merged(parts):
        parts = [part.astype(F32) for part in parts]
        stats = [part[8:16] for part in parts]
        tops = [
            jnp.broadcast_to(stat[:, 0:1] + stat[:, 32:33], (8, 128)) for stat in stats
        ]
        totals = [jnp.broadcast_to(stat[:, 64:65], (8, 128)) for stat in stats]
        top = tops[0]
        for t in tops[1:]:
            top = jnp.maximum(top, t)
        high = top.astype(BF16).astype(F32)
        low = (top - high).astype(BF16).astype(F32)
        total = jnp.zeros((8, 128), F32)
        result = jnp.zeros((8, 128), F32)
        for t, s, part in zip(tops, totals, parts):
            factor = jnp.exp(t - (high + low))
            total += s * factor
            result += part[0:8] * factor
        return high, low, total, result

    loads[7].wait()
    loads[8].wait()
    bundle(6, agq.at[0:15]).wait_recv()
    position = lax.broadcasted_iota(jnp.int32, (8, 256), 1) + seq * 256
    each = range(16)
    scores = [
        lax.dot_general(agq[r], kc[r], (((1,), (1,)), ((), ())), preferred_element_type=F32)
        * scale
        for r in each
    ]
    valid = [position < lengths[r] for r in each]
    scores = [jnp.where(valid[r], scores[r], masked_score) for r in each]
    tops = [jnp.max(scores[r], axis=1, keepdims=True) for r in each]
    highs = [top.astype(BF16).astype(F32) for top in tops]
    lows = [(top - high).astype(BF16).astype(F32) for top, high in zip(tops, highs)]
    weights = [
        jnp.where(valid[r], jnp.exp(scores[r] - (highs[r] + lows[r])), 0.0) for r in each
    ]
    totals = [jnp.sum(weights[r], axis=1, keepdims=True) for r in each]
    results = [
        jnp.dot(weights[r].astype(BF16), vc[r], preferred_element_type=F32) for r in each
    ]
    for r in each:
        rso_src[r] = packed(highs[r], lows[r], totals[r], results[r])
    for k, (dy, dz) in enumerate(WINDOW):
        send(7, rso_src.at[row_of(dy, dz)], rso.at[k], (dy, dz, 0))

    bundle(7, rso).wait_recv()
    z2o[0] = packed(*merged([rso_src[mine]] + [rso[k] for k in range(15)]))
    for k, dz in enumerate(QUARTER):
        send(8, z2o.at[0], z2o.at[k + 1], (0, dz, 0))
    bundle(8, z2o.at[1:4]).wait_recv()
    high, low, total, result = merged([z2o[k] for k in range(4)])
    top = high + low
    peak = jnp.maximum(top, own_score)
    factor = jnp.exp(top - peak)
    own_weight = jnp.exp(own_score - peak)
    attended = (result * factor + own_weight * value_own) / (total * factor + own_weight)
    ago[mine] = attended.astype(BF16)
    for dy, dz in WINDOW:
        send(9, ago.at[mine], ago.at[mine], (dy, dz, 0))

    loads[9].wait()
    bundle(9, ago.at[0:15]).wait_recv()
    flat[0:128, :] = ago[...].astype(F32).reshape(128, 128)
    projected = jnp.zeros((16, 128), F32)
    for j in range(8):
        projected += jnp.dot(
            flat[pl.ds(j, 16, stride=8), :].astype(BF16),
            wo[j * 128 : (j + 1) * 128, :],
            preferred_element_type=F32,
        )
    hbuf[0] = projected.astype(BF16)
    for k, dh in enumerate(HEADS):
        send(10, hbuf.at[0], hbuf.at[k + 1], (0, 0, dh))
    bundle(10, hbuf.at[1:8]).wait_recv()
    out[...] = jnp.sum(hbuf[...].astype(F32), axis=0).astype(BF16)

    for stage, view in enumerate(
        [t1a.at[1:32], t1b.at[1:16], rsb, z2b.at[1:4], rse, z2e.at[1:4], agq.at[0:15], rso,
         z2o.at[1:4], ago.at[0:15], hbuf.at[1:8]]
    ):
        bundle(stage, view).wait_send()


def body(hid, gain, wq, wk, wv, wo, down, up, choice, lengths, kc, vc):
    anywhere = pl.BlockSpec(memory_space=pl.ANY)
    return pl.pallas_call(
        kernel,
        out_shape=pltpu.VMEM((16, 128), BF16),
        in_specs=[anywhere] * 12,
        out_specs=pl.BlockSpec(memory_space=pltpu.VMEM),
        scratch_shapes=[
            pltpu.VMEM((16, 128), BF16),
            pltpu.VMEM((1, 128), BF16),
            pltpu.VMEM((128, 1024), BF16),
            pltpu.VMEM((128, 128), BF16),
            pltpu.VMEM((128, 128), BF16),
            pltpu.VMEM((1024, 128), BF16),
            pltpu.VMEM((1024, 128), BF16),
            pltpu.VMEM((128, 1024), BF16),
            pltpu.VMEM((16, 256, 128), BF16),
            pltpu.VMEM((16, 256, 128), BF16),
            pltpu.SMEM((16,), jnp.int32),
            pltpu.SMEM((16,), jnp.int32),
            pltpu.VMEM((32, 2, 128), F32),
            pltpu.VMEM((16, 2, 128), F32),
            pltpu.VMEM((256, 128), F32),
            pltpu.VMEM((16, 16, 128), BF16),
            pltpu.VMEM((15, 16, 128), BF16),
            pltpu.VMEM((4, 16, 128), BF16),
            pltpu.VMEM((16, 8, 128), BF16),
            pltpu.VMEM((15, 8, 128), BF16),
            pltpu.VMEM((4, 8, 128), BF16),
            pltpu.VMEM((16, 8, 128), BF16),
            pltpu.VMEM((16, 16, 128), BF16),
            pltpu.VMEM((15, 16, 128), BF16),
            pltpu.VMEM((4, 16, 128), BF16),
            pltpu.VMEM((16, 8, 128), BF16),
            pltpu.VMEM((8, 16, 128), BF16),
            pltpu.SemaphoreType.DMA((12,)),
            pltpu.SemaphoreType.DMA((STAGES,)),
            pltpu.SemaphoreType.DMA((STAGES,)),
            pltpu.SemaphoreType.REGULAR,
        ],
        compiler_params=pltpu.CompilerParams(collective_id=0, has_side_effects=True),
    )(
        hid, gain.reshape(1, 128), wq, wk, wv, wo, down.reshape(1024, 128), up.reshape(128, 1024),
        choice, lengths, kc.reshape(16, 256, 128), vc.reshape(16, 256, 128),
    )


def solution(mesh):
    placed = (
        P(None, "seq"),
        P("seq"),
        P("seq", "head"),
        P("seq", "head"),
        P("seq", "head"),
        P("head", "seq"),
        P("head", None, "seq"),
        P("seq", None, "head"),
        P(),
        P(),
        P(None, "seq", "head", None),
        P(None, "seq", "head", None),
    )
    return jax.shard_map(
        body, mesh=mesh, in_specs=placed, out_specs=P(None, "seq"), check_vma=False
    )
```

time: 75.3 us -> 65.4 us (0.87)
  Pallas kernels: 73.9 us -> 64.7 us
    pallas_call x1, Pallas kernels: 73.9 us -> 64.7 us  [body(): pl.pallas_call(kernel, out_shape=pltpu.VMEM((16, 128), BF16), in_specs=[a...]
where the time goes in v2:
time: 65.4 us; the launch traced here: 65.3 us
  Pallas kernels  64.7 us (99%)
    pallas_call x1, Pallas kernels, body(): pl.pallas_call(kernel, out_shape=pltpu.VMEM((16, 128), BF16), in_specs=[a...  64.7 us

profile of v2, /device:TPU:1, one launch (start us, length us, event | category | flops | bytes accessed | tf_op | source)
XLA Modules:
  0.0 65.3 jit_solution(14154754537125611075)
XLA Ops:
  0.0 64.7 %shard_map.118 = bf16[16,128]{1,0:T(8,128)(2,1)S(1)} custom-call(bf16[16,128]{1,0:T(8,128)(2,1)} %hid_h.1, bf16[1,128]{1,0:T(2,128)(2,1)} %bitcast.9, bf16[128,1024]{1,0:T(8,128)(2,1)} %wq_h.1, bf16[128,128]{1,0:T(8,128)(2,1)} %wk_h.1, bf16[128,128]{1,0:T(8,128)(2,1)} %wv_h.1, bf16[1024,128]{1,0:T(8,128)(2,1)} %wo_h.1, bf16[1024,128]{1,0:T(8,128)(2,1)} %bitcast.7, ...), custom_call_target="tpu_custom_call" | custom-call | tf_op jit(solution)/shard_map/pallas_call | solution.py:288
  64.7 0.6 copy.14

commit v3 on v2

--- a/solution.py
+++ b/solution.py
@@ -16,8 +16,9 @@
 NY, NZ, NH = 4, 16, 8
 PLANE = [(dy, dh) for dy in range(NY) for dh in range(NH) if (dy, dh) != (0, 0)]
 COLUMN = list(range(1, NZ))
-WINDOW = [(dy, dz) for dz in (2, -1, 1, 0) for dy in (2, 1, 3, 0) if (dy, dz) != (0, 0)]
-QUARTER = [8, 4, 12]
+WINDOW = [(dy, dz) for dy in (2, 1, 3) for dz in (2 if dy == 2 else -2, 1, -1, 0)]
+WINDOW += [(0, 2), (0, 1), (0, -1)]
+QUARTER = [6, -6, 2, -2]
 HEADS = list(range(1, NH))
 NEAR = [1, -1, 2, -2, 3, -3, 4, -4]
 STAGES = 11
@@ -27,7 +28,7 @@
     hid_h, gain_h, wq_h, wk_h, wv_h, wo_h, down_h, up_h, choice_h, lengths_h, kc_h, vc_h,
     out,
     hid, gain, wq, wk, wv, wo, down, up, kc, vc, choice, lengths,
-    t1a, t1b, flat, rsb_src, rsb, z2b, rse_src, rse, z2e, agq, rso_src, rso, z2o, ago, hbuf,
+    t1a, t1b, flat, rsb_src, rsb, z2b, ups_src, ups, z2e, agq, rso_src, rso, z2o, ago, hbuf,
     load_sem, send_sem, recv_sem, vouch,
 ):
     seq = lax.axis_index("seq")
@@ -35,18 +36,12 @@
     y = lax.rem(seq, NY)
     z = lax.div(seq, NY)
     mine = y * 4 + lax.rem(z, 4)
+    first = y * 4 + lax.rem(z + 2, 4)
 
     def at(dy, dz, dh):
         yy = lax.rem(y + (dy + NY) % NY, NY)
         zz = lax.rem(z + (dz + NZ) % NZ, NZ)
         return (zz * NY + yy, lax.rem(head + (dh + NH) % NH, NH))
-
-    barrier = pltpu.get_barrier_semaphore()
-    greeted = [(0, dz, 0) for dz in NEAR]
-    greeted += [(-dy, -dz, 0) for dy, dz in WINDOW if dy and dz]
-    greeted += [(dy, 0, dh) for dy, dh in PLANE]
-    for dy, dz, dh in greeted:
-        pl.semaphore_signal(barrier, inc=1, device_id=at(dy, dz, dh), device_id_type=MESH)
 
     loads = [
         pltpu.make_async_copy(src, dst, load_sem.at[k])
@@ -56,8 +51,15 @@
              (lengths_h, lengths)]
         )
     ]
-    for c in loads:
-        c.start()
+    for k in (10, 0, 1, 2, 6, 3, 4, 5, 7, 8, 9, 11):
+        loads[k].start()
+
+    barrier = pltpu.get_barrier_semaphore()
+    greeted = [(0, dz, 0) for dz in NEAR]
+    greeted += [(-dy, -dz, 0) for dy, dz in WINDOW if dy and dz]
+    greeted += [(dy, 0, dh) for dy, dh in PLANE]
+    for dy, dz, dh in greeted:
+        pl.semaphore_signal(barrier, inc=1, device_id=at(dy, dz, dh), device_id_type=MESH)
 
     def send(stage, src, dst, where):
         pltpu.make_async_remote_copy(
@@ -100,11 +102,14 @@
     t1a[0, 0:1, :] = jnp.sum(diagonal[0:8], axis=0, keepdims=True)
     t1a[0, 1:2, :] = jnp.sum(diagonal[8:16], axis=0, keepdims=True)
 
-    pl.semaphore_wait(barrier, len(greeted))
-    for k, (dy, dh) in enumerate(PLANE):
-        send(0, t1a.at[0], t1a.at[k + 1], (dy, 0, dh))
-    for dz in (4, -4):
-        pl.semaphore_signal(vouch, inc=1, device_id=at(0, dz, 0), device_id_type=MESH)
+    loads[6].wait()
+    for r in range(16):
+        local = choice[r] - seq * 8
+        found = up[jnp.clip(local, 0, 7)]
+        here = (chosen[r : r + 1] >= seq * 8) & (chosen[r : r + 1] < seq * 8 + 8)
+        here = jnp.broadcast_to(jnp.where(here, 1.0, 0.0), (16, 128)).astype(BF16)
+        for j in range(8):
+            ups_src[r, :, j * 128 : (j + 1) * 128] = found[:, j * 128 : (j + 1) * 128] * here
 
     for c in loads[3:6]:
         c.wait()
@@ -120,11 +125,19 @@
         flat[pl.ds(j, 16, stride=16), :] = jnp.zeros((16, 128), F32)
     rsb_src[...] = flat[...].reshape(16, 16, 128).astype(BF16)
 
+    pl.semaphore_wait(barrier, len(greeted))
+    for k, (dy, dh) in enumerate(PLANE):
+        send(0, t1a.at[0], t1a.at[k + 1], (dy, 0, dh))
+    for dz in (4, -4):
+        pl.semaphore_signal(vouch, inc=1, device_id=at(0, dz, 0), device_id_type=MESH)
+
     def row_of(dy, dz):
-        return lax.rem(y + dy, 4) * 4 + lax.rem(lax.rem(z, 4) + dz + 4, 4)
+        return lax.rem(y + dy, 4) * 4 + lax.rem(z + dz + 6, 4)
 
     for k, (dy, dz) in enumerate(WINDOW):
         send(2, rsb_src.at[row_of(dy, dz)], rsb.at[k], (dy, dz, 0))
+    for k, (dy, dz) in enumerate(WINDOW):
+        send(4, ups_src.at[row_of(dy, dz)], ups.at[k], (dy, dz, 0))
 
     bundle(0, t1a.at[1:32]).wait_recv()
     t1b[0] = jnp.sum(t1a[...], axis=0)
@@ -133,7 +146,7 @@
         send(1, t1b.at[0], t1b.at[k + 1], (0, dz, 0))
 
     bundle(2, rsb).wait_recv()
-    base = rsb_src[mine].astype(F32)
+    base = rsb_src[first].astype(F32)
     for k in range(15):
         base += rsb[k].astype(F32)
     z2b[0] = base.astype(BF16)
@@ -148,44 +161,38 @@
     sine = jnp.sin(angle)
     sine = jnp.where(lane8 < 64, -sine, sine)
 
-    loads[6].wait()
+    bundle(4, ups).wait_recv()
+    up_rows = ups_src[first]
+    for k in range(15):
+        up_rows += ups[k]
     bundle(1, t1b.at[1:16]).wait_recv()
     whole = jnp.sum(t1b[...], axis=0)
-    spread = jnp.concatenate(
-        [jnp.broadcast_to(whole[0:1], (8, 128)), jnp.broadcast_to(whole[1:2], (8, 128))], axis=0
-    )
-    spread = jnp.where(group == rows8, spread, 0.0)
-    for shift in (64, 32, 16):
-        spread += pltpu.roll(spread, shift, 1)
-    placed = jnp.where(chosen == seq * 8 + group, spread, 0.0).astype(BF16)
-    expand = jnp.dot(placed, up[...], preferred_element_type=F32)
+    ranks = jnp.where(first < 8, whole[0:1], whole[1:2])
+    ranks = pltpu.roll(ranks, lax.rem(128 - 16 * lax.rem(first, 8), 128), 1)
+    ranks = jnp.broadcast_to(ranks, (8, 128)).astype(BF16)
+    expand = jnp.dot(ranks[:, 0:16], up_rows, preferred_element_type=F32)
+    sub8 = lax.broadcasted_iota(jnp.int32, (8, 128), 0)
+    grown = jnp.zeros((8, 128), F32)
     for j in range(8):
-        flat[pl.ds(j, 16, stride=8), :] = expand[:, j * 128 : (j + 1) * 128]
-    rse_src[...] = flat[0:128, :].reshape(16, 8, 128).astype(BF16)
-    for k, (dy, dz) in enumerate(WINDOW):
-        send(4, rse_src.at[row_of(dy, dz)], rse.at[k], (dy, dz, 0))
-
-    bundle(3, z2b.at[1:4]).wait_recv()
-    base = z2b[0].astype(F32)
-    for k in range(1, 4):
-        base += z2b[k].astype(F32)
-    inverse = lax.rsqrt(base[10:11] * (1.0 / 8192.0) + norm_epsilon)
-    bundle(4, rse).wait_recv()
-    grown = rse_src[mine].astype(F32)
-    for k in range(15):
-        grown += rse[k].astype(F32)
+        grown += jnp.where(sub8 == j, expand[:, j * 128 : (j + 1) * 128], 0.0)
     z2e[0] = grown.astype(BF16)
     for k, dz in enumerate(QUARTER):
         send(5, z2e.at[0], z2e.at[k + 1], (0, dz, 0))
 
+    bundle(3, z2b.at[1:5]).wait_recv()
+    base = z2b[1].astype(F32)
+    for k in range(2, 5):
+        base += z2b[k].astype(F32)
+    inverse = lax.rsqrt(base[10:11] * (1.0 / 8192.0) + norm_epsilon)
+
     def rotated(x):
         return (x * cosine + pltpu.roll(x, 64, 1) * sine).astype(BF16)
 
     key_rot = rotated(jnp.broadcast_to(base[8:9] * inverse, (8, 128))).astype(F32)
     value_own = jnp.broadcast_to(base[9:10] * inverse, (8, 128)).astype(BF16).astype(F32)
-    bundle(5, z2e.at[1:4]).wait_recv()
+    bundle(5, z2e.at[1:5]).wait_recv()
     query = base[0:8]
-    for k in range(4):
+    for k in range(1, 5):
         query += z2e[k].astype(F32)
     query_rot = rotated(query * inverse)
     agq[mine] = query_rot
@@ -246,11 +253,11 @@
         send(7, rso_src.at[row_of(dy, dz)], rso.at[k], (dy, dz, 0))
 
     bundle(7, rso).wait_recv()
-    z2o[0] = packed(*merged([rso_src[mine]] + [rso[k] for k in range(15)]))
+    z2o[0] = packed(*merged([rso_src[first]] + [rso[k] for k in range(15)]))
     for k, dz in enumerate(QUARTER):
         send(8, z2o.at[0], z2o.at[k + 1], (0, dz, 0))
-    bundle(8, z2o.at[1:4]).wait_recv()
-    high, low, total, result = merged([z2o[k] for k in range(4)])
+    bundle(8, z2o.at[1:5]).wait_recv()
+    high, low, total, result = merged([z2o[k] for k in range(1, 5)])
     top = high + low
     peak = jnp.maximum(top, own_score)
     factor = jnp.exp(top - peak)
@@ -277,8 +284,8 @@
     out[...] = jnp.sum(hbuf[...].astype(F32), axis=0).astype(BF16)
 
     for stage, view in enumerate(
-        [t1a.at[1:32], t1b.at[1:16], rsb, z2b.at[1:4], rse, z2e.at[1:4], agq.at[0:15], rso,
-         z2o.at[1:4], ago.at[0:15], hbuf.at[1:8]]
+        [t1a.at[1:32], t1b.at[1:16], rsb, z2b.at[1:5], ups, z2e.at[1:5], agq.at[0:15], rso,
+         z2o.at[1:5], ago.at[0:15], hbuf.at[1:8]]
     ):
         bundle(stage, view).wait_send()
 
@@ -298,7 +305,7 @@
             pltpu.VMEM((128, 128), BF16),
             pltpu.VMEM((1024, 128), BF16),
             pltpu.VMEM((1024, 128), BF16),
-            pltpu.VMEM((128, 1024), BF16),
+            pltpu.VMEM((8, 16, 1024), BF16),
             pltpu.VMEM((16, 256, 128), BF16),
             pltpu.VMEM((16, 256, 128), BF16),
             pltpu.SMEM((16,), jnp.int32),
@@ -308,14 +315,14 @@
             pltpu.VMEM((256, 128), F32),
             pltpu.VMEM((16, 16, 128), BF16),
             pltpu.VMEM((15, 16, 128), BF16),
-            pltpu.VMEM((4, 16, 128), BF16),
-            pltpu.VMEM((16, 8, 128), BF16),
-            pltpu.VMEM((15, 8, 128), BF16),
-            pltpu.VMEM((4, 8, 128), BF16),
+            pltpu.VMEM((5, 16, 128), BF16),
+            pltpu.VMEM((16, 16, 1024), BF16),
+            pltpu.VMEM((15, 16, 1024), BF16),
+            pltpu.VMEM((5, 8, 128), BF16),
             pltpu.VMEM((16, 8, 128), BF16),
             pltpu.VMEM((16, 16, 128), BF16),
             pltpu.VMEM((15, 16, 128), BF16),
-            pltpu.VMEM((4, 16, 128), BF16),
+            pltpu.VMEM((5, 16, 128), BF16),
             pltpu.VMEM((16, 8, 128), BF16),
             pltpu.VMEM((8, 16, 128), BF16),
             pltpu.SemaphoreType.DMA((12,)),
@@ -325,7 +332,7 @@
         ],
         compiler_params=pltpu.CompilerParams(collective_id=0, has_side_effects=True),
     )(
-        hid, gain.reshape(1, 128), wq, wk, wv, wo, down.reshape(1024, 128), up.reshape(128, 1024),
+        hid, gain.reshape(1, 128), wq, wk, wv, wo, down.reshape(1024, 128), up,
         choice, lengths, kc.reshape(16, 256, 128), vc.reshape(16, 256, 128),
     )
 

time: 65.4 us -> 62.9 us (0.962)
  Pallas kernels: 64.7 us -> 62.1 us
    pallas_call x1, Pallas kernels: 64.7 us -> 62.1 us  [body(): pl.pallas_call(kernel, out_shape=pltpu.VMEM((16, 128), BF16), in_specs=[a...]
where the time goes in v3:
time: 62.9 us; the launch traced here: 62.8 us
  Pallas kernels  62.1 us (99%)
    pallas_call x1, Pallas kernels, body(): pl.pallas_call(kernel, out_shape=pltpu.VMEM((16, 128), BF16), in_specs=[a...  62.1 us

profile of v3, /device:TPU:1, one launch (start us, length us, event | category | flops | bytes accessed | tf_op | source)
XLA Modules:
  0.0 62.8 jit_solution(8157694819705729220)
XLA Ops:
  0.0 62.1 %shard_map.118 = bf16[16,128]{1,0:T(8,128)(2,1)S(1)} custom-call(bf16[16,128]{1,0:T(8,128)(2,1)} %hid_h.1, bf16[1,128]{1,0:T(2,128)(2,1)} %bitcast.7, bf16[128,1024]{1,0:T(8,128)(2,1)} %wq_h.1, bf16[128,128]{1,0:T(8,128)(2,1)} %wk_h.1, bf16[128,128]{1,0:T(8,128)(2,1)} %wv_h.1, bf16[1024,128]{1,0:T(8,128)(2,1)} %wo_h.1, bf16[1024,128]{1,0:T(8,128)(2,1)} %bitcast.6, ...), custom_call_target="tpu_custom_call" | custom-call | tf_op jit(solution)/shard_map/pallas_call | solution.py:295
  62.2 0.6 copy.14

commit v4 on v3

--- a/solution.py
+++ b/solution.py
@@ -16,9 +16,9 @@
 NY, NZ, NH = 4, 16, 8
 PLANE = [(dy, dh) for dy in range(NY) for dh in range(NH) if (dy, dh) != (0, 0)]
 COLUMN = list(range(1, NZ))
-WINDOW = [(dy, dz) for dy in (2, 1, 3) for dz in (2 if dy == 2 else -2, 1, -1, 0)]
-WINDOW += [(0, 2), (0, 1), (0, -1)]
-QUARTER = [6, -6, 2, -2]
+WINDOW = [(2, 1), (2, -1), (-1, 2), (-1, -2), (2, 0), (1, 1), (1, -1), (-1, 1), (-1, -1)]
+WINDOW += [(0, 2), (0, -2), (1, 0), (-1, 0), (0, 1), (0, -1)]
+QUARTER = [(-1, 6), (1, -6), (1, 2), (-1, -2)]
 HEADS = list(range(1, NH))
 NEAR = [1, -1, 2, -2, 3, -3, 4, -4]
 STAGES = 11
@@ -35,8 +35,13 @@
     head = lax.axis_index("head")
     y = lax.rem(seq, NY)
     z = lax.div(seq, NY)
-    mine = y * 4 + lax.rem(z, 4)
-    first = y * 4 + lax.rem(z + 2, 4)
+
+    def owned(dy, dz):
+        zz = lax.rem(z + dz + NZ, NZ)
+        return lax.rem(y + dy + NY + 2 * lax.div(zz, 4), 4) * 4 + lax.rem(zz, 4)
+
+    mine = owned(0, 0)
+    first = owned(1, 2)
 
     def at(dy, dz, dh):
         yy = lax.rem(y + (dy + NY) % NY, NY)
@@ -57,6 +62,7 @@
     barrier = pltpu.get_barrier_semaphore()
     greeted = [(0, dz, 0) for dz in NEAR]
     greeted += [(-dy, -dz, 0) for dy, dz in WINDOW if dy and dz]
+    greeted += [(-1, 2, 0), (-1, -2, 0)]
     greeted += [(dy, 0, dh) for dy, dh in PLANE]
     for dy, dz, dh in greeted:
         pl.semaphore_signal(barrier, inc=1, device_id=at(dy, dz, dh), device_id_type=MESH)
@@ -132,7 +138,7 @@
         pl.semaphore_signal(vouch, inc=1, device_id=at(0, dz, 0), device_id_type=MESH)
 
     def row_of(dy, dz):
-        return lax.rem(y + dy, 4) * 4 + lax.rem(z + dz + 6, 4)
+        return owned(dy + 1, dz + 2)
 
     for k, (dy, dz) in enumerate(WINDOW):
         send(2, rsb_src.at[row_of(dy, dz)], rsb.at[k], (dy, dz, 0))
@@ -150,8 +156,8 @@
     for k in range(15):
         base += rsb[k].astype(F32)
     z2b[0] = base.astype(BF16)
-    for k, dz in enumerate(QUARTER):
-        send(3, z2b.at[0], z2b.at[k + 1], (0, dz, 0))
+    for k, (dy, dz) in enumerate(QUARTER):
+        send(3, z2b.at[0], z2b.at[k + 1], (dy, dz, 0))
 
     loads[11].wait()
     half = lax.rem(lane8, 64).astype(F32)
@@ -176,8 +182,8 @@
     for j in range(8):
         grown += jnp.where(sub8 == j, expand[:, j * 128 : (j + 1) * 128], 0.0)
     z2e[0] = grown.astype(BF16)
-    for k, dz in enumerate(QUARTER):
-        send(5, z2e.at[0], z2e.at[k + 1], (0, dz, 0))
+    for k, (dy, dz) in enumerate(QUARTER):
+        send(5, z2e.at[0], z2e.at[k + 1], (dy, dz, 0))
 
     bundle(3, z2b.at[1:5]).wait_recv()
     base = z2b[1].astype(F32)
@@ -254,8 +260,8 @@
 
     bundle(7, rso).wait_recv()
     z2o[0] = packed(*merged([rso_src[first]] + [rso[k] for k in range(15)]))
-    for k, dz in enumerate(QUARTER):
-        send(8, z2o.at[0], z2o.at[k + 1], (0, dz, 0))
+    for k, (dy, dz) in enumerate(QUARTER):
+        send(8, z2o.at[0], z2o.at[k + 1], (dy, dz, 0))
     bundle(8, z2o.at[1:5]).wait_recv()
     high, low, total, result = merged([z2o[k] for k in range(1, 5)])
     top = high + low

time: 62.9 us -> 63.7 us (1.013)
  Pallas kernels: 62.1 us -> 63 us
    pallas_call x1, Pallas kernels: 62.1 us -> 63 us  [body(): pl.pallas_call(kernel, out_shape=pltpu.VMEM((16, 128), BF16), in_specs=[a...]
where the time goes in v4:
time: 63.7 us; the launch traced here: 63.6 us
  Pallas kernels  63 us (99%)
    pallas_call x1, Pallas kernels, body(): pl.pallas_call(kernel, out_shape=pltpu.VMEM((16, 128), BF16), in_specs=[a...  63 us

profile of v4, /device:TPU:1, one launch (start us, length us, event | category | flops | bytes accessed | tf_op | source)
XLA Modules:
  0.0 63.6 jit_solution(10128662923062548195)
XLA Ops:
  0.0 63.0 %shard_map.118 = bf16[16,128]{1,0:T(8,128)(2,1)S(1)} custom-call(bf16[16,128]{1,0:T(8,128)(2,1)} %hid_h.1, bf16[1,128]{1,0:T(2,128)(2,1)} %bitcast.7, bf16[128,1024]{1,0:T(8,128)(2,1)} %wq_h.1, bf16[128,128]{1,0:T(8,128)(2,1)} %wk_h.1, bf16[128,128]{1,0:T(8,128)(2,1)} %wv_h.1, bf16[1024,128]{1,0:T(8,128)(2,1)} %wo_h.1, bf16[1024,128]{1,0:T(8,128)(2,1)} %bitcast.6, ...), custom_call_target="tpu_custom_call" | custom-call | tf_op jit(solution)/shard_map/pallas_call | solution.py:301
  63.0 0.6 copy.14

commit v5 on v3

--- a/solution.py
+++ b/solution.py
@@ -21,14 +21,14 @@
 QUARTER = [6, -6, 2, -2]
 HEADS = list(range(1, NH))
 NEAR = [1, -1, 2, -2, 3, -3, 4, -4]
-STAGES = 11
+STAGES = 12
 
 
 def kernel(
     hid_h, gain_h, wq_h, wk_h, wv_h, wo_h, down_h, up_h, choice_h, lengths_h, kc_h, vc_h,
     out,
     hid, gain, wq, wk, wv, wo, down, up, kc, vc, choice, lengths,
-    t1a, t1b, flat, rsb_src, rsb, z2b, ups_src, ups, z2e, agq, rso_src, rso, z2o, ago, hbuf,
+    t1a, t1b, flat, rsb_src, rsb, z2b, ups_src, ups, ups_y, z2e, agq, rso_src, rso, z2o, ago, hbuf,
     load_sem, send_sem, recv_sem, vouch,
 ):
     seq = lax.axis_index("seq")
@@ -109,7 +109,7 @@
         here = (chosen[r : r + 1] >= seq * 8) & (chosen[r : r + 1] < seq * 8 + 8)
         here = jnp.broadcast_to(jnp.where(here, 1.0, 0.0), (16, 128)).astype(BF16)
         for j in range(8):
-            ups_src[r, :, j * 128 : (j + 1) * 128] = found[:, j * 128 : (j + 1) * 128] * here
+            ups_src[r % 4, r // 4, :, j * 128 : (j + 1) * 128] = found[:, j * 128 : (j + 1) * 128] * here
 
     for c in loads[3:6]:
         c.wait()
@@ -136,8 +136,9 @@
 
     for k, (dy, dz) in enumerate(WINDOW):
         send(2, rsb_src.at[row_of(dy, dz)], rsb.at[k], (dy, dz, 0))
-    for k, (dy, dz) in enumerate(WINDOW):
-        send(4, ups_src.at[row_of(dy, dz)], ups.at[k], (dy, dz, 0))
+    for dz, k, low, high in ((2, 2, 0, 2), (-2, 2, 2, 4), (1, 0, 0, 4), (-1, 1, 0, 4)):
+        part = ups_src.at[lax.rem(z + dz + 2, 4), low:high]
+        send(4, part, ups.at[k, low:high], (0, dz, 0))
 
     bundle(0, t1a.at[1:32]).wait_recv()
     t1b[0] = jnp.sum(t1a[...], axis=0)
@@ -153,6 +154,11 @@
     for k, dz in enumerate(QUARTER):
         send(3, z2b.at[0], z2b.at[k + 1], (0, dz, 0))
 
+    bundle(4, ups).wait_recv()
+    ups_y[0] = (ups_src[lax.rem(z + 2, 4)] + ups[0]) + (ups[1] + ups[2])
+    for dy in (2, 1, 3):
+        send(11, ups_y.at[0, lax.rem(y + dy, 4)], ups_y.at[1, dy], (dy, 0, 0))
+
     loads[11].wait()
     half = lax.rem(lane8, 64).astype(F32)
     frequency = jnp.exp(-half * (jnp.log(jnp.full((8, 128), rope_base, F32)) / 64.0))
@@ -161,10 +167,8 @@
     sine = jnp.sin(angle)
     sine = jnp.where(lane8 < 64, -sine, sine)
 
-    bundle(4, ups).wait_recv()
-    up_rows = ups_src[first]
-    for k in range(15):
-        up_rows += ups[k]
+    bundle(11, ups_y.at[1, 1:4]).wait_recv()
+    up_rows = (ups_y[0, y] + ups_y[1, 1]) + (ups_y[1, 2] + ups_y[1, 3])
     bundle(1, t1b.at[1:16]).wait_recv()
     whole = jnp.sum(t1b[...], axis=0)
     ranks = jnp.where(first < 8, whole[0:1], whole[1:2])
@@ -285,7 +289,8 @@
 
     for stage, view in enumerate(
         [t1a.at[1:32], t1b.at[1:16], rsb, z2b.at[1:5], ups, z2e.at[1:5], agq.at[0:15], rso,
-         z2o.at[1:5], ago.at[0:15], hbuf.at[1:8]]
+         z2o.at[1:5], ago.at[0:15], hbuf.at[1:8],
+         ups_y.at[1, 1:4]]
     ):
         bundle(stage, view).wait_send()
 
@@ -316,8 +321,9 @@
             pltpu.VMEM((16, 16, 128), BF16),
             pltpu.VMEM((15, 16, 128), BF16),
             pltpu.VMEM((5, 16, 128), BF16),
-            pltpu.VMEM((16, 16, 1024), BF16),
-            pltpu.VMEM((15, 16, 1024), BF16),
+            pltpu.VMEM((4, 4, 16, 1024), BF16),
+            pltpu.VMEM((3, 4, 16, 1024), BF16),
+            pltpu.VMEM((2, 4, 16, 1024), BF16),
             pltpu.VMEM((5, 8, 128), BF16),
             pltpu.VMEM((16, 8, 128), BF16),
             pltpu.VMEM((16, 16, 128), BF16),

time: 62.9 us -> 61.1 us (0.971)
  Pallas kernels: 62.1 us -> 60.4 us
    pallas_call x1, Pallas kernels: 62.1 us -> 60.4 us  [body(): pl.pallas_call(kernel, out_shape=pltpu.VMEM((16, 128), BF16), in_specs=[a...]
where the time goes in v5:
time: 61.1 us; the launch traced here: 61 us
  Pallas kernels  60.4 us (99%)
    pallas_call x1, Pallas kernels, body(): pl.pallas_call(kernel, out_shape=pltpu.VMEM((16, 128), BF16), in_specs=[a...  60.4 us

profile of v5, /device:TPU:1, one launch (start us, length us, event | category | flops | bytes accessed | tf_op | source)
XLA Modules:
  0.0 61.0 jit_solution(2341795397670253169)
XLA Ops:
  0.0 60.4 %shard_map.118 = bf16[16,128]{1,0:T(8,128)(2,1)S(1)} custom-call(bf16[16,128]{1,0:T(8,128)(2,1)} %hid_h.1, bf16[1,128]{1,0:T(2,128)(2,1)} %bitcast.7, bf16[128,1024]{1,0:T(8,128)(2,1)} %wq_h.1, bf16[128,128]{1,0:T(8,128)(2,1)} %wk_h.1, bf16[128,128]{1,0:T(8,128)(2,1)} %wv_h.1, bf16[1024,128]{1,0:T(8,128)(2,1)} %wo_h.1, bf16[1024,128]{1,0:T(8,128)(2,1)} %bitcast.6, ...), custom_call_target="tpu_custom_call" | custom-call | tf_op jit(solution)/shard_map/pallas_call | solution.py:300
  60.4 0.6 copy.14

commit v6 on v5

--- a/solution.py
+++ b/solution.py
@@ -21,18 +21,19 @@
 QUARTER = [6, -6, 2, -2]
 HEADS = list(range(1, NH))
 NEAR = [1, -1, 2, -2, 3, -3, 4, -4]
-STAGES = 12
+STAGES = 15
 
 
 def kernel(
     hid_h, gain_h, wq_h, wk_h, wv_h, wo_h, down_h, up_h, choice_h, lengths_h, kc_h, vc_h,
     out,
     hid, gain, wq, wk, wv, wo, down, up, kc, vc, choice, lengths,
-    t1a, t1b, flat, rsb_src, rsb, z2b, ups_src, ups, ups_y, z2e, agq, rso_src, rso, z2o, ago, hbuf,
+    t1a, t1b, flat, rsb_src, rsb, z2b, ups_src, ups, ups_y, z2e, agq, rso_src, rso, z2o, own_src, own_in, ago_src, ago, hbuf,
     load_sem, send_sem, recv_sem, vouch,
 ):
     seq = lax.axis_index("seq")
     head = lax.axis_index("head")
+    core = lax.rem(head, 2)
     y = lax.rem(seq, NY)
     z = lax.div(seq, NY)
     mine = y * 4 + lax.rem(z, 4)
@@ -204,6 +205,12 @@
         send(6, agq.at[mine], agq.at[mine], (dy, dz, 0))
     scale = 128.0**-0.5
     own_score = jnp.sum(query_rot.astype(F32) * key_rot, axis=1, keepdims=True) * scale
+    own_src[0:8, :] = jnp.broadcast_to(own_score, (8, 128))
+    own_src[8:16, :] = value_own
+
+    @pl.when(core == 0)
+    def _():
+        send(12, own_src, own_in, (0, 0, 1))
 
     def packed(high, low, total, result):
         stat = jnp.where(lane8 < 32, high, jnp.where(lane8 < 64, low, total))
@@ -253,26 +260,45 @@
     ]
     for r in each:
         rso_src[r] = packed(highs[r], lows[r], totals[r], results[r])
-    for k, (dy, dz) in enumerate(WINDOW):
-        send(7, rso_src.at[row_of(dy, dz)], rso.at[k], (dy, dz, 0))
-
-    bundle(7, rso).wait_recv()
-    z2o[0] = packed(*merged([rso_src[first]] + [rso[k] for k in range(15)]))
-    for k, dz in enumerate(QUARTER):
-        send(8, z2o.at[0], z2o.at[k + 1], (0, dz, 0))
-    bundle(8, z2o.at[1:5]).wait_recv()
-    high, low, total, result = merged([z2o[k] for k in range(1, 5)])
-    top = high + low
-    peak = jnp.maximum(top, own_score)
-    factor = jnp.exp(top - peak)
-    own_weight = jnp.exp(own_score - peak)
-    attended = (result * factor + own_weight * value_own) / (total * factor + own_weight)
-    ago[mine] = attended.astype(BF16)
-    for dy, dz in WINDOW:
-        send(9, ago.at[mine], ago.at[mine], (dy, dz, 0))
+    @pl.when(core == 0)
+    def _():
+        for k, (dy, dz) in enumerate(WINDOW):
+            send(7, rso_src.at[row_of(dy, dz)], rso.at[k], (dy, dz, 1))
+        send(7, rso_src.at[first], rso.at[15], (0, 0, 1))
+        bundle(13, ago).wait_recv()
+
+    @pl.when(core == 1)
+    def _():
+        for k, (dy, dz) in enumerate(WINDOW):
+            send(14, rso_src.at[row_of(dy, dz)], rso.at[k + 16], (dy, dz, 0))
+
+        bundle(7, rso.at[0:16]).wait_recv()
+        z2o[0, 0] = packed(*merged([rso[k] for k in range(16)]))
+        bundle(14, rso.at[16:31]).wait_recv()
+        z2o[0, 1] = packed(*merged([rso_src[first]] + [rso[k] for k in range(16, 31)]))
+        for k, dz in enumerate(QUARTER):
+            send(8, z2o.at[0], z2o.at[k + 1], (0, dz, 0))
+
+        def attended(slot, own_score, value_own):
+            high, low, total, result = merged([z2o[k, slot] for k in range(1, 5)])
+            top = high + low
+            peak = jnp.maximum(top, own_score)
+            factor = jnp.exp(top - peak)
+            own_weight = jnp.exp(own_score - peak)
+            summed = result * factor + own_weight * value_own
+            return (summed / (total * factor + own_weight)).astype(BF16)
+
+        bundle(12, own_in).wait_recv()
+        bundle(8, z2o.at[1:5]).wait_recv()
+        ago_src[...] = attended(0, own_in[0:8, :], own_in[8:16, :])
+        ago[mine] = attended(1, own_src[0:8, :], own_src[8:16, :])
+        for dy, dz in WINDOW:
+            send(13, ago_src, ago.at[mine], (dy, dz, -1))
+            send(9, ago.at[mine], ago.at[mine], (dy, dz, 0))
+        send(13, ago_src, ago.at[mine], (0, 0, -1))
+        bundle(9, ago.at[0:15]).wait_recv()
 
     loads[9].wait()
-    bundle(9, ago.at[0:15]).wait_recv()
     flat[0:128, :] = ago[...].astype(F32).reshape(128, 128)
     projected = jnp.zeros((16, 128), F32)
     for j in range(8):
@@ -287,12 +313,24 @@
     bundle(10, hbuf.at[1:8]).wait_recv()
     out[...] = jnp.sum(hbuf[...].astype(F32), axis=0).astype(BF16)
 
-    for stage, view in enumerate(
-        [t1a.at[1:32], t1b.at[1:16], rsb, z2b.at[1:5], ups, z2e.at[1:5], agq.at[0:15], rso,
-         z2o.at[1:5], ago.at[0:15], hbuf.at[1:8],
-         ups_y.at[1, 1:4]]
-    ):
+    sent = [
+        (0, t1a.at[1:32]), (1, t1b.at[1:16]), (2, rsb), (3, z2b.at[1:5]), (4, ups),
+        (5, z2e.at[1:5]), (6, agq.at[0:15]), (10, hbuf.at[1:8]), (11, ups_y.at[1, 1:4]),
+    ]
+    for stage, view in sent:
         bundle(stage, view).wait_send()
+
+    @pl.when(core == 0)
+    def _():
+        bundle(12, own_in).wait_send()
+        bundle(7, rso.at[0:16]).wait_send()
+
+    @pl.when(core == 1)
+    def _():
+        bundle(14, rso.at[16:31]).wait_send()
+        bundle(8, z2o.at[1:5]).wait_send()
+        bundle(13, ago).wait_send()
+        bundle(9, ago.at[0:15]).wait_send()
 
 
 def body(hid, gain, wq, wk, wv, wo, down, up, choice, lengths, kc, vc):
@@ -327,8 +365,11 @@
             pltpu.VMEM((5, 8, 128), BF16),
             pltpu.VMEM((16, 8, 128), BF16),
             pltpu.VMEM((16, 16, 128), BF16),
-            pltpu.VMEM((15, 16, 128), BF16),
-            pltpu.VMEM((5, 16, 128), BF16),
+            pltpu.VMEM((31, 16, 128), BF16),
+            pltpu.VMEM((5, 2, 16, 128), BF16),
+            pltpu.VMEM((16, 128), F32),
+            pltpu.VMEM((16, 128), F32),
+            pltpu.VMEM((8, 128), BF16),
             pltpu.VMEM((16, 8, 128), BF16),
             pltpu.VMEM((8, 16, 128), BF16),
             pltpu.SemaphoreType.DMA((12,)),

time: 61.1 us -> 59.7 us (0.977)
  Pallas kernels: 60.4 us -> 59 us
    pallas_call x1, Pallas kernels: 60.4 us -> 59 us  [body(): pl.pallas_call(kernel, out_shape=pltpu.VMEM((16, 128), BF16), in_specs=[a...]
where the time goes in v6:
time: 59.7 us; the launch traced here: 59.6 us
  Pallas kernels  59 us (99%)
  local copies, waits for them, and re-layouts  0.6 us (1%)
    pallas_call x1, Pallas kernels, body(): pl.pallas_call(kernel, out_shape=pltpu.VMEM((16, 128), BF16), in_specs=[a...  59 us

profile of v6, /device:TPU:1, one launch (start us, length us, event | category | flops | bytes accessed | tf_op | source)
XLA Modules:
  0.0 59.6 jit_solution(10468001461224049194)
XLA Ops:
  0.0 59.0 %shard_map.118 = bf16[16,128]{1,0:T(8,128)(2,1)S(1)} custom-call(bf16[16,128]{1,0:T(8,128)(2,1)} %hid_h.1, bf16[1,128]{1,0:T(2,128)(2,1)} %bitcast.7, bf16[128,1024]{1,0:T(8,128)(2,1)} %wq_h.1, bf16[128,128]{1,0:T(8,128)(2,1)} %wk_h.1, bf16[128,128]{1,0:T(8,128)(2,1)} %wv_h.1, bf16[1024,128]{1,0:T(8,128)(2,1)} %wo_h.1, bf16[1024,128]{1,0:T(8,128)(2,1)} %bitcast.6, ...), custom_call_target="tpu_custom_call" | custom-call | tf_op jit(solution)/shard_map/pallas_call | solution.py:338
  59.0 0.6 copy.14

commit v7 on v6

--- a/solution.py
+++ b/solution.py
@@ -14,21 +14,21 @@
 masked_score = -1e30
 
 NY, NZ, NH = 4, 16, 8
-PLANE = [(dy, dh) for dy in range(NY) for dh in range(NH) if (dy, dh) != (0, 0)]
+PLANE = [(dy, dh) for dy in (2, 1, 3, 0) for dh in range(NH) if (dy, dh) != (0, 0)]
 COLUMN = list(range(1, NZ))
 WINDOW = [(dy, dz) for dy in (2, 1, 3) for dz in (2 if dy == 2 else -2, 1, -1, 0)]
 WINDOW += [(0, 2), (0, 1), (0, -1)]
 QUARTER = [6, -6, 2, -2]
 HEADS = list(range(1, NH))
 NEAR = [1, -1, 2, -2, 3, -3, 4, -4]
-STAGES = 15
+STAGES = 18
 
 
 def kernel(
     hid_h, gain_h, wq_h, wk_h, wv_h, wo_h, down_h, up_h, choice_h, lengths_h, kc_h, vc_h,
     out,
     hid, gain, wq, wk, wv, wo, down, up, kc, vc, choice, lengths,
-    t1a, t1b, flat, rsb_src, rsb, z2b, ups_src, ups, ups_y, z2e, agq, rso_src, rso, z2o, own_src, own_in, ago_src, ago, hbuf,
+    t1_src, t1a, t1b, flat, rsb_src, rsb, z2b, ups_src, ups, ups_y, ups_in, z2e, agq_src, agq, rso_src, rso, z2o, own_src, own_in, own, ago_src, ago, hbuf,
     load_sem, send_sem, recv_sem, vouch,
 ):
     seq = lax.axis_index("seq")
@@ -42,7 +42,7 @@
     def at(dy, dz, dh):
         yy = lax.rem(y + (dy + NY) % NY, NY)
         zz = lax.rem(z + (dz + NZ) % NZ, NZ)
-        return (zz * NY + yy, lax.rem(head + (dh + NH) % NH, NH))
+        return (zz * NY + yy, lax.rem(head + dh + NH, NH))
 
     loads = [
         pltpu.make_async_copy(src, dst, load_sem.at[k])
@@ -56,9 +56,9 @@
         loads[k].start()
 
     barrier = pltpu.get_barrier_semaphore()
-    greeted = [(0, dz, 0) for dz in NEAR]
+    greeted = [(dy, 0, dh) for dy, dh in PLANE]
+    greeted += [(0, dz, 0) for dz in NEAR]
     greeted += [(-dy, -dz, 0) for dy, dz in WINDOW if dy and dz]
-    greeted += [(dy, 0, dh) for dy, dh in PLANE]
     for dy, dz, dh in greeted:
         pl.semaphore_signal(barrier, inc=1, device_id=at(dy, dz, dh), device_id_type=MESH)
 
@@ -100,8 +100,8 @@
         fold += pltpu.roll(fold, shift, 1)
     diagonal = jnp.where(group == rows8, fold, 0.0)
     square = jnp.sum(values * values, axis=1, keepdims=True)
-    t1a[0, 0:1, :] = jnp.sum(diagonal[0:8], axis=0, keepdims=True)
-    t1a[0, 1:2, :] = jnp.sum(diagonal[8:16], axis=0, keepdims=True)
+    t1_src[0:1, :] = jnp.sum(diagonal[0:8], axis=0, keepdims=True)
+    t1_src[1:2, :] = jnp.sum(diagonal[8:16], axis=0, keepdims=True)
 
     loads[6].wait()
     for r in range(16):
@@ -127,8 +127,18 @@
     rsb_src[...] = flat[...].reshape(16, 16, 128).astype(BF16)
 
     pl.semaphore_wait(barrier, len(greeted))
-    for k, (dy, dh) in enumerate(PLANE):
-        send(0, t1a.at[0], t1a.at[k + 1], (dy, 0, dh))
+    for dy in (2, 1, 3, 0):
+        for dx in (2, 1, 3, 0):
+            if (dy, dx) != (0, 0):
+                send(0, t1_src, t1a.at[(dy * 4 + dx) * 2 + core], (dy, 0, 2 * dx + 1 - core))
+
+    @pl.when(core == 0)
+    def _():
+        send(17, t1_src, t1a.at[0], (0, 0, 1))
+
+    @pl.when(core == 1)
+    def _():
+        t1a[1] = t1_src[...]
     for dz in (4, -4):
         pl.semaphore_signal(vouch, inc=1, device_id=at(0, dz, 0), device_id_type=MESH)
 
@@ -141,11 +151,15 @@
         part = ups_src.at[lax.rem(z + dz + 2, 4), low:high]
         send(4, part, ups.at[k, low:high], (0, dz, 0))
 
-    bundle(0, t1a.at[1:32]).wait_recv()
-    t1b[0] = jnp.sum(t1a[...], axis=0)
     pl.semaphore_wait(vouch, 2)
-    for k, dz in enumerate(COLUMN):
-        send(1, t1b.at[0], t1b.at[k + 1], (0, dz, 0))
+
+    @pl.when(core == 1)
+    def _():
+        bundle(0, t1a.at[2:32]).wait_recv()
+        bundle(17, t1a.at[0]).wait_recv()
+        t1b[0] = jnp.sum(t1a[...], axis=0)
+        for k, dz in enumerate(COLUMN):
+            send(1, t1b.at[0], t1b.at[k + 1], (0, dz, 0))
 
     bundle(2, rsb).wait_recv()
     base = rsb_src[first].astype(F32)
@@ -156,9 +170,18 @@
         send(3, z2b.at[0], z2b.at[k + 1], (0, dz, 0))
 
     bundle(4, ups).wait_recv()
-    ups_y[0] = (ups_src[lax.rem(z + 2, 4)] + ups[0]) + (ups[1] + ups[2])
-    for dy in (2, 1, 3):
-        send(11, ups_y.at[0, lax.rem(y + dy, 4)], ups_y.at[1, dy], (dy, 0, 0))
+    ups_y[...] = (ups_src[lax.rem(z + 2, 4)] + ups[0]) + (ups[1] + ups[2])
+
+    @pl.when(core == 0)
+    def _():
+        for k, dy in enumerate((2, 1, 3)):
+            send(15, ups_y.at[lax.rem(y + dy, 4)], ups_in.at[k], (dy, 0, 1))
+        send(15, ups_y.at[y], ups_in.at[3], (0, 0, 1))
+
+    @pl.when(core == 1)
+    def _():
+        for k, dy in enumerate((2, 1, 3)):
+            send(11, ups_y.at[lax.rem(y + dy, 4)], ups_in.at[k + 4], (dy, 0, 0))
 
     loads[11].wait()
     half = lax.rem(lane8, 64).astype(F32)
@@ -168,49 +191,69 @@
     sine = jnp.sin(angle)
     sine = jnp.where(lane8 < 64, -sine, sine)
 
-    bundle(11, ups_y.at[1, 1:4]).wait_recv()
-    up_rows = (ups_y[0, y] + ups_y[1, 1]) + (ups_y[1, 2] + ups_y[1, 3])
-    bundle(1, t1b.at[1:16]).wait_recv()
-    whole = jnp.sum(t1b[...], axis=0)
-    ranks = jnp.where(first < 8, whole[0:1], whole[1:2])
-    ranks = pltpu.roll(ranks, lax.rem(128 - 16 * lax.rem(first, 8), 128), 1)
-    ranks = jnp.broadcast_to(ranks, (8, 128)).astype(BF16)
-    expand = jnp.dot(ranks[:, 0:16], up_rows, preferred_element_type=F32)
-    sub8 = lax.broadcasted_iota(jnp.int32, (8, 128), 0)
-    grown = jnp.zeros((8, 128), F32)
-    for j in range(8):
-        grown += jnp.where(sub8 == j, expand[:, j * 128 : (j + 1) * 128], 0.0)
-    z2e[0] = grown.astype(BF16)
-    for k, dz in enumerate(QUARTER):
-        send(5, z2e.at[0], z2e.at[k + 1], (0, dz, 0))
-
-    bundle(3, z2b.at[1:5]).wait_recv()
-    base = z2b[1].astype(F32)
-    for k in range(2, 5):
-        base += z2b[k].astype(F32)
-    inverse = lax.rsqrt(base[10:11] * (1.0 / 8192.0) + norm_epsilon)
-
     def rotated(x):
         return (x * cosine + pltpu.roll(x, 64, 1) * sine).astype(BF16)
 
-    key_rot = rotated(jnp.broadcast_to(base[8:9] * inverse, (8, 128))).astype(F32)
-    value_own = jnp.broadcast_to(base[9:10] * inverse, (8, 128)).astype(BF16).astype(F32)
-    bundle(5, z2e.at[1:5]).wait_recv()
-    query = base[0:8]
-    for k in range(1, 5):
-        query += z2e[k].astype(F32)
-    query_rot = rotated(query * inverse)
-    agq[mine] = query_rot
-    for dy, dz in WINDOW:
-        send(6, agq.at[mine], agq.at[mine], (dy, dz, 0))
+    def sum_base():
+        bundle(3, z2b.at[1:5]).wait_recv()
+        base = z2b[1].astype(F32)
+        for k in range(2, 5):
+            base += z2b[k].astype(F32)
+        own_src[...] = base
+
     scale = 128.0**-0.5
-    own_score = jnp.sum(query_rot.astype(F32) * key_rot, axis=1, keepdims=True) * scale
-    own_src[0:8, :] = jnp.broadcast_to(own_score, (8, 128))
-    own_src[8:16, :] = value_own
 
     @pl.when(core == 0)
     def _():
+        sum_base()
         send(12, own_src, own_in, (0, 0, 1))
+        bundle(16, agq).wait_recv()
+
+    @pl.when(core == 1)
+    def _():
+        bundle(11, ups_in.at[4:7]).wait_recv()
+        bundle(15, ups_in.at[0:4]).wait_recv()
+        up_even = (ups_in[0] + ups_in[1]) + (ups_in[2] + ups_in[3])
+        up_odd = (ups_y[y] + ups_in[4]) + (ups_in[5] + ups_in[6])
+        bundle(1, t1b.at[1:16]).wait_recv()
+        whole = jnp.sum(t1b[...], axis=0)
+        ranks = jnp.where(first < 8, whole[0:1], whole[1:2])
+        ranks = pltpu.roll(ranks, lax.rem(128 - 16 * lax.rem(first, 8), 128), 1)
+        ranks = jnp.broadcast_to(ranks, (8, 128)).astype(BF16)
+        sub8 = lax.broadcasted_iota(jnp.int32, (8, 128), 0)
+        for slot, up_rows in enumerate((up_even, up_odd)):
+            expand = jnp.dot(ranks[:, 0:16], up_rows, preferred_element_type=F32)
+            grown = jnp.zeros((8, 128), F32)
+            for j in range(8):
+                grown += jnp.where(sub8 == j, expand[:, j * 128 : (j + 1) * 128], 0.0)
+            z2e[0, slot] = grown.astype(BF16)
+        for k, dz in enumerate(QUARTER):
+            send(5, z2e.at[0], z2e.at[k + 1], (0, dz, 0))
+
+        sum_base()
+        bundle(12, own_in).wait_recv()
+        bases = (own_in[...], own_src[...])
+        inverses = [lax.rsqrt(base[10:11] * (1.0 / 8192.0) + norm_epsilon) for base in bases]
+        bundle(5, z2e.at[1:5]).wait_recv()
+        queries = []
+        for slot, (base, inverse) in enumerate(zip(bases, inverses)):
+            query = base[0:8]
+            for k in range(1, 5):
+                query += z2e[k, slot].astype(F32)
+            queries.append(rotated(query * inverse))
+        agq_src[...] = queries[0]
+        agq[mine] = queries[1]
+        for dy, dz in WINDOW:
+            send(16, agq_src, agq.at[mine], (dy, dz, -1))
+            send(6, agq.at[mine], agq.at[mine], (dy, dz, 0))
+        send(16, agq_src, agq.at[mine], (0, 0, -1))
+        for slot, (base, inverse) in enumerate(zip(bases, inverses)):
+            key_rot = rotated(jnp.broadcast_to(base[8:9] * inverse, (8, 128))).astype(F32)
+            value_own = jnp.broadcast_to(base[9:10] * inverse, (8, 128)).astype(BF16)
+            own_score = jnp.sum(queries[slot].astype(F32) * key_rot, axis=1, keepdims=True)
+            own[slot, 0:8, :] = jnp.broadcast_to(own_score * scale, (8, 128))
+            own[slot, 8:16, :] = value_own.astype(F32)
+        bundle(6, agq.at[0:15]).wait_recv()
 
     def packed(high, low, total, result):
         stat = jnp.where(lane8 < 32, high, jnp.where(lane8 < 64, low, total))
@@ -238,7 +281,6 @@
 
     loads[7].wait()
     loads[8].wait()
-    bundle(6, agq.at[0:15]).wait_recv()
     position = lax.broadcasted_iota(jnp.int32, (8, 256), 1) + seq * 256
     each = range(16)
     scores = [
@@ -288,10 +330,9 @@
             summed = result * factor + own_weight * value_own
             return (summed / (total * factor + own_weight)).astype(BF16)
 
-        bundle(12, own_in).wait_recv()
         bundle(8, z2o.at[1:5]).wait_recv()
-        ago_src[...] = attended(0, own_in[0:8, :], own_in[8:16, :])
-        ago[mine] = attended(1, own_src[0:8, :], own_src[8:16, :])
+        ago_src[...] = attended(0, own[0, 0:8, :], own[0, 8:16, :])
+        ago[mine] = attended(1, own[1, 0:8, :], own[1, 8:16, :])
         for dy, dz in WINDOW:
             send(13, ago_src, ago.at[mine], (dy, dz, -1))
             send(9, ago.at[mine], ago.at[mine], (dy, dz, 0))
@@ -314,19 +355,25 @@
     out[...] = jnp.sum(hbuf[...].astype(F32), axis=0).astype(BF16)
 
     sent = [
-        (0, t1a.at[1:32]), (1, t1b.at[1:16]), (2, rsb), (3, z2b.at[1:5]), (4, ups),
-        (5, z2e.at[1:5]), (6, agq.at[0:15]), (10, hbuf.at[1:8]), (11, ups_y.at[1, 1:4]),
+        (0, t1a.at[0:15]), (2, rsb), (3, z2b.at[1:5]), (4, ups), (10, hbuf.at[1:8]),
     ]
     for stage, view in sent:
         bundle(stage, view).wait_send()
 
     @pl.when(core == 0)
     def _():
+        bundle(17, t1_src).wait_send()
         bundle(12, own_in).wait_send()
+        bundle(15, ups_in.at[0:4]).wait_send()
         bundle(7, rso.at[0:16]).wait_send()
 
     @pl.when(core == 1)
     def _():
+        bundle(1, t1b.at[1:16]).wait_send()
+        bundle(11, ups_in.at[4:7]).wait_send()
+        bundle(5, z2e.at[1:5]).wait_send()
+        bundle(16, agq).wait_send()
+        bundle(6, agq.at[0:15]).wait_send()
         bundle(14, rso.at[16:31]).wait_send()
         bundle(8, z2o.at[1:5]).wait_send()
         bundle(13, ago).wait_send()
@@ -353,6 +400,7 @@
             pltpu.VMEM((16, 256, 128), BF16),
             pltpu.SMEM((16,), jnp.int32),
             pltpu.SMEM((16,), jnp.int32),
+            pltpu.VMEM((2, 128), F32),
             pltpu.VMEM((32, 2, 128), F32),
             pltpu.VMEM((16, 2, 128), F32),
             pltpu.VMEM((256, 128), F32),
@@ -361,14 +409,17 @@
             pltpu.VMEM((5, 16, 128), BF16),
             pltpu.VMEM((4, 4, 16, 1024), BF16),
             pltpu.VMEM((3, 4, 16, 1024), BF16),
-            pltpu.VMEM((2, 4, 16, 1024), BF16),
-            pltpu.VMEM((5, 8, 128), BF16),
+            pltpu.VMEM((4, 16, 1024), BF16),
+            pltpu.VMEM((7, 16, 1024), BF16),
+            pltpu.VMEM((5, 2, 8, 128), BF16),
+            pltpu.VMEM((8, 128), BF16),
             pltpu.VMEM((16, 8, 128), BF16),
             pltpu.VMEM((16, 16, 128), BF16),
             pltpu.VMEM((31, 16, 128), BF16),
             pltpu.VMEM((5, 2, 16, 128), BF16),
             pltpu.VMEM((16, 128), F32),
             pltpu.VMEM((16, 128), F32),
+            pltpu.VMEM((2, 16, 128), F32),
             pltpu.VMEM((8, 128), BF16),
             pltpu.VMEM((16, 8, 128), BF16),
             pltpu.VMEM((8, 16, 128), BF16),

time: 59.7 us -> 57.8 us (0.968)
  Pallas kernels: 59 us -> 57.1 us
    pallas_call x1, Pallas kernels: 59 us -> 57.1 us  [body(): pl.pallas_call(kernel, out_shape=pltpu.VMEM((16, 128), BF16), in_specs=[a...]
where the time goes in v7:
time: 57.8 us; the launch traced here: 57.7 us
  Pallas kernels  57.1 us (99%)
  local copies, waits for them, and re-layouts  0.6 us (1%)
    pallas_call x1, Pallas kernels, body(): pl.pallas_call(kernel, out_shape=pltpu.VMEM((16, 128), BF16), in_specs=[a...  57.1 us

profile of v7, /device:TPU:1, one launch (start us, length us, event | category | flops | bytes accessed | tf_op | source)
XLA Modules:
  0.0 57.7 jit_solution(10472802106177809970)
XLA Ops:
  0.0 57.1 %shard_map.118 = bf16[16,128]{1,0:T(8,128)(2,1)S(1)} custom-call(bf16[16,128]{1,0:T(8,128)(2,1)} %hid_h.1, bf16[1,128]{1,0:T(2,128)(2,1)} %bitcast.7, bf16[128,1024]{1,0:T(8,128)(2,1)} %wq_h.1, bf16[128,128]{1,0:T(8,128)(2,1)} %wk_h.1, bf16[128,128]{1,0:T(8,128)(2,1)} %wv_h.1, bf16[1024,128]{1,0:T(8,128)(2,1)} %wo_h.1, bf16[1024,128]{1,0:T(8,128)(2,1)} %bitcast.6, ...), custom_call_target="tpu_custom_call" | custom-call | tf_op jit(solution)/shard_map/pallas_call | solution.py:385
  57.1 0.6 %copy.14 = bf16[16,128]{1,0:T(8,128)(2,1)} copy(bf16[16,128]{1,0:T(8,128)(2,1)S(1)} %shard_map.118) | data formatting | bytes 8192

commit v8 on v7

--- a/solution.py
+++ b/solution.py
@@ -145,11 +145,11 @@
     def row_of(dy, dz):
         return lax.rem(y + dy, 4) * 4 + lax.rem(z + dz + 6, 4)
 
-    for k, (dy, dz) in enumerate(WINDOW):
-        send(2, rsb_src.at[row_of(dy, dz)], rsb.at[k], (dy, dz, 0))
     for dz, k, low, high in ((2, 2, 0, 2), (-2, 2, 2, 4), (1, 0, 0, 4), (-1, 1, 0, 4)):
         part = ups_src.at[lax.rem(z + dz + 2, 4), low:high]
         send(4, part, ups.at[k, low:high], (0, dz, 0))
+    for k, (dy, dz) in enumerate(WINDOW):
+        send(2, rsb_src.at[row_of(dy, dz)], rsb.at[k], (dy, dz, 0))
 
     pl.semaphore_wait(vouch, 2)
 

time: 57.8 us -> 59.2 us (1.024)
  Pallas kernels: 57.1 us -> 58.5 us
    pallas_call x1, Pallas kernels: 57.1 us -> 58.5 us  [body(): pl.pallas_call(kernel, out_shape=pltpu.VMEM((16, 128), BF16), in_specs=[a...]
where the time goes in v8:
time: 59.2 us; the launch traced here: 59.1 us
  Pallas kernels  58.5 us (99%)
  local copies, waits for them, and re-layouts  0.6 us (1%)
    pallas_call x1, Pallas kernels, body(): pl.pallas_call(kernel, out_shape=pltpu.VMEM((16, 128), BF16), in_specs=[a...  58.5 us

profile of v8, /device:TPU:1, one launch (start us, length us, event | category | flops | bytes accessed | tf_op | source)
XLA Modules:
  0.0 59.1 jit_solution(12601853939210278103)
XLA Ops:
  0.0 58.5 %shard_map.118 = bf16[16,128]{1,0:T(8,128)(2,1)S(1)} custom-call(bf16[16,128]{1,0:T(8,128)(2,1)} %hid_h.1, bf16[1,128]{1,0:T(2,128)(2,1)} %bitcast.7, bf16[128,1024]{1,0:T(8,128)(2,1)} %wq_h.1, bf16[128,128]{1,0:T(8,128)(2,1)} %wk_h.1, bf16[128,128]{1,0:T(8,128)(2,1)} %wv_h.1, bf16[1024,128]{1,0:T(8,128)(2,1)} %wo_h.1, bf16[1024,128]{1,0:T(8,128)(2,1)} %bitcast.6, ...), custom_call_target="tpu_custom_call" | custom-call | tf_op jit(solution)/shard_map/pallas_call | solution.py:385
  58.5 0.6 %copy.14 = bf16[16,128]{1,0:T(8,128)(2,1)} copy(bf16[16,128]{1,0:T(8,128)(2,1)S(1)} %shard_map.118) | data formatting | bytes 8192
